TPU v7x, 128 devices: a whole 4x4x4 slice. The times are simulated.
128 devices in a mesh: ctx: 8 (over z_hi, x), tp: 8 (over y, core), ep: 2 (over z_lo).
Axes of the slice: x: 4, y: 4, z: 4 (z_hi: 2, z_lo: 2; z = z_hi * 2 + z_lo), core: 2. Of those that a mesh axis runs over, the one named last changes fastest.
Arguments:
- resid: bfloat16 [2048, 6144], P('ctx', ('tp', 'ep')), may hold values from -60 to 60
- queries: bfloat16 [2048, 6144], P('ctx', 'tp'), may hold values from -6 to 6
- keys: bfloat16 [2048, 1024], P('ctx', 'tp'), may hold values from -4 to 4
- values: bfloat16 [2048, 1024], P('ctx', 'tp'), may hold values from -5 to 5
- w_out: bfloat16 [6144, 6144], P('tp', ('ctx', 'ep')), may hold values from -0.078125 to 0.078125
- norm_gain: bfloat16 [6144], P(('tp', 'ep')), may hold values from 0.5 to 1.5
- w_gate: bfloat16 [8, 6144, 8192], P('tp', None, ('ctx', 'ep')), may hold values from -0.078125 to 0.078125
- w_up: bfloat16 [8, 6144, 8192], P('tp', None, ('ctx', 'ep')), may hold values from -0.078125 to 0.078125
- w_down: bfloat16 [8, 8192, 6144], P('tp', ('ctx', 'ep')), may hold values from -0.0625 to 0.0625
- expert_ids: int32 [2048, 2], P('ctx'), may hold values from 0 to 7, all different within a row; in each aligned block of 256 rows (0 to 255, 256 to 511, ...) at most 96 rows name the same one
- route_units: int32 [2048, 2], P('ctx'), may hold values from 1 to 65535
Outputs:
- mixed: bfloat16 [2048, 6144], P('ctx', ('tp', 'ep'))
Inputs may be any that keep to these rules, and one draw needn't show every extreme that they name: `expert_ids`: each row names two different experts; in every aligned block of 256 rows no expert is named by more than 96 rows, a bound that some block reaches.
All inputs are finite; a program needn't handle non-finite values.
Results may differ from a plain program's by a relative error of at most 0.01.
Values may be sent and summed in bfloat16 or wider, within the bound.
A program may use at most 128 MiB of HBM per device.

v0:
```python
import jax
import jax.numpy as jnp
from jax import lax
from jax.sharding import Mesh
from jax.sharding import PartitionSpec as P

D = 6144
HD = 128
TP = ("tp_0", "tp_1")
TP_EP = ("tp_0", "tp_1", "ep")


def split_up(x, dim, size):
    dims = x.shape
    tiles = x.reshape(*dims[:dim], size, dims[dim] // size, *dims[dim + 1 :])
    return jnp.moveaxis(tiles, dim, 0)


def sent_and_summed(x, axis, dim):
    tiles = split_up(x, dim, lax.axis_size(axis))
    arrived = lax.all_to_all(tiles, axis, split_axis=0, concat_axis=0, tiled=True)
    return arrived.astype(jnp.float32).sum(axis=0)


def from_everyone(x, axis):
    size = lax.axis_size(axis)
    return lax.all_to_all(jnp.broadcast_to(x[None], (size, *x.shape)), axis, 0, 0, tiled=True)


def taken_together(x, axis):
    everything = from_everyone(x, axis)
    return jnp.sum(everything, axis=0)


def laid_out(tiles, dim):
    dims = list(tiles.shape[1:])
    dims[dim] *= tiles.shape[0]
    return jnp.moveaxis(tiles, 0, dim).reshape(dims)


def moved_by_axis(tiles, axes, sequence):
    dims = [lax.axis_size(a) for a in axes]
    tiles = tiles.reshape(*dims, *tiles.shape[1:])
    for k in sequence:
        tiles = lax.all_to_all(tiles, axes[k], split_axis=k, concat_axis=k, tiled=True)
    return tiles.reshape(-1, *tiles.shape[len(axes) :])


def one_axis_at_a_time(x, axes, sequence, split_dim, concat_dim):
    tiles = split_up(x, split_dim, lax.axis_size(axes))
    return laid_out(moved_by_axis(tiles, axes, sequence), concat_dim)


def from_partner(x, axis, distance):
    return lax.ppermute(x, axis, [(i, i ^ 1 << distance) for i in range(lax.axis_size(axis))])


def on_device(
    resid, queries, keys, values, w_out, norm_gain, w_gate, w_up, w_down, expert_ids, route_units
):
    tp_size = lax.axis_size(TP)
    ep_size = lax.axis_size("ep")
    ctx_size = lax.axis_size("ctx")
    tok_rows = queries.shape[0]
    heads_dev = queries.shape[1] // HD
    kv_dev = keys.shape[1] // HD
    group = heads_dev // kv_dev
    feat_dev = resid.shape[1]
    hidden_dev = w_gate.shape[2]
    capacity = 3 * tok_rows // tp_size
    first_pos = lax.axis_index("ctx") * tok_rows
    query_heads = queries.reshape(tok_rows, kv_dev, group, HD)
    query_pos = first_pos + jnp.arange(tok_rows, dtype=jnp.int32)
    running_max = jnp.full((kv_dev, group, tok_rows), -1e30, jnp.float32)
    key_piece = lax.all_gather(keys, "ctx", axis=0, tiled=True)
    value_piece = lax.all_gather(values, "ctx", axis=0, tiled=True)
    count = key_piece.shape[0]
    key_rows = key_piece.reshape(count, kv_dev, HD)
    value_rows = value_piece.reshape(count, kv_dev, HD)
    scores = jnp.einsum(
        "tkgd,nkd->kgtn", query_heads, key_rows, preferred_element_type=jnp.float32
    ) * HD ** (-0.5)
    key_pos = jnp.arange(count, dtype=jnp.int32)
    allowed = (key_pos[None, :] <= query_pos[:, None])[None, None]
    block_max = jnp.max(jnp.where(allowed, scores, -1e30), axis=-1)
    new_max = jnp.maximum(running_max, block_max)
    probs = jnp.where(allowed, jnp.exp(scores - new_max[..., None]), 0.0)
    new_sum = jnp.sum(probs, axis=-1)
    probs_b = probs.astype(jnp.bfloat16)
    update = jnp.einsum("kgtn,nkd->kgtd", probs_b, value_rows, preferred_element_type=jnp.float32)
    attn = (
        (update / new_sum[..., None])
        .transpose(2, 0, 1, 3)
        .reshape(tok_rows, heads_dev * HD)
        .astype(jnp.bfloat16)
    )
    partial_proj = jnp.dot(
        attn, lax.all_gather(w_out, "ctx", axis=1, tiled=True), preferred_element_type=jnp.float32
    )
    proj = sent_and_summed(partial_proj.astype(jnp.bfloat16), TP, 1)
    hres = (resid.astype(jnp.float32) + proj).astype(jnp.bfloat16)
    hfloat = hres.astype(jnp.float32)
    square_total = taken_together(jnp.sum(hfloat * hfloat, axis=1, keepdims=True), TP_EP)
    normed = (hfloat * lax.rsqrt(square_total / D + 1e-05) * norm_gain.astype(jnp.float32)).astype(
        jnp.bfloat16
    )
    onehot = (expert_ids[..., None] == jnp.arange(tp_size, dtype=jnp.int32)).astype(jnp.int32)
    per_token = jnp.sum(onehot, axis=1)
    earlier = jnp.cumsum(per_token, axis=0) - per_token
    slot = jnp.sum(onehot * earlier[:, None, :], axis=-1)
    codes = expert_ids * capacity + slot
    slot_ids = jnp.arange(tp_size * capacity, dtype=jnp.int32)
    picks = (
        (slot_ids[:, None] == codes[None, :, 0]) | (slot_ids[:, None] == codes[None, :, 1])
    ).astype(jnp.bfloat16)
    dispatched = jnp.dot(picks, normed, preferred_element_type=jnp.float32).astype(jnp.bfloat16)
    dispatched = dispatched.reshape(tp_size, 1, capacity, feat_dev)
    arrived = one_axis_at_a_time(dispatched, TP, (1, 0), 0, 1)
    gate_w = w_gate[0].reshape(tp_size, ep_size, feat_dev, hidden_dev)
    up_w = w_up[0].reshape(tp_size, ep_size, feat_dev, hidden_dev)
    zero_acc = jnp.zeros((ctx_size, capacity, hidden_dev), jnp.float32)
    piece = lax.all_gather(arrived, ("ctx", "ep"), axis=0, tiled=True)

    def one_row(index, totals):
        gate_total, up_total = totals
        source = index // ep_size
        parity = index % ep_size
        row = lax.dynamic_index_in_dim(piece, index, 0, keepdims=False)
        gate_part = lax.dynamic_index_in_dim(gate_w, parity, 1, keepdims=False)
        up_part = lax.dynamic_index_in_dim(up_w, parity, 1, keepdims=False)
        gate_add = jnp.einsum("tsj,tjf->sf", row, gate_part, preferred_element_type=jnp.float32)
        up_add = jnp.einsum("tsj,tjf->sf", row, up_part, preferred_element_type=jnp.float32)
        gate_now = lax.dynamic_index_in_dim(gate_total, source, 0, keepdims=False) + gate_add
        up_now = lax.dynamic_index_in_dim(up_total, source, 0, keepdims=False) + up_add
        return (
            lax.dynamic_update_index_in_dim(gate_total, gate_now, source, 0),
            lax.dynamic_update_index_in_dim(up_total, up_now, source, 0),
        )

    gate_acc, up_acc = lax.fori_loop(0, piece.shape[0], one_row, (zero_acc, zero_acc))
    hidden = (jax.nn.silu(gate_acc) * up_acc).astype(jnp.bfloat16)
    down_w = w_down[0].reshape(hidden_dev, tp_size, ep_size, feat_dev)
    parity = lax.axis_index("ep")
    mine_cols = lax.dynamic_index_in_dim(down_w, parity, 2, keepdims=False)
    give_cols = lax.dynamic_index_in_dim(down_w, 1 - parity, 2, keepdims=False)
    got_hidden, got_cols = from_partner((hidden, give_cols), "ep", 0)
    hidden_both = jnp.concatenate([hidden, got_hidden], axis=2)
    cols_both = jnp.concatenate([mine_cols, got_cols], axis=0)
    blocks = lax.axis_size("ctx") * capacity // capacity
    product = jnp.einsum(
        "csf,ftj->cstj", hidden_both, cols_both, preferred_element_type=jnp.float32
    )
    expert_sum = lax.psum_scatter(
        product.reshape(blocks * capacity, tp_size * feat_dev).astype(jnp.bfloat16),
        "ctx",
        scatter_dimension=0,
        tiled=True,
    )
    expert_out = expert_sum.reshape(1, capacity, tp_size, feat_dev)
    returned = lax.all_to_all(expert_out, TP, split_axis=2, concat_axis=0, tiled=True)
    units = route_units.astype(jnp.float32)
    weights = (units / jnp.sum(units, axis=-1, keepdims=True)).astype(jnp.bfloat16)
    combine = jnp.where(slot_ids[None, :] == codes[:, 0:1], weights[:, 0:1], 0.0) + jnp.where(
        slot_ids[None, :] == codes[:, 1:2], weights[:, 1:2], 0.0
    )
    moe = jnp.dot(
        combine, returned.reshape(tp_size * capacity, feat_dev), preferred_element_type=jnp.float32
    )
    return (hfloat + moe).astype(jnp.bfloat16)


def solution(mesh):
    torus = Mesh(
        mesh.devices.reshape(mesh.shape["ctx"], 4, 2, mesh.shape["ep"]),
        ("ctx", "tp_0", "tp_1", "ep"),
    )
    in_specs = (
        P("ctx", TP_EP),
        P("ctx", TP),
        P("ctx", TP),
        P("ctx", TP),
        P(TP, ("ctx", "ep")),
        P(TP_EP),
        P(TP, None, ("ctx", "ep")),
        P(TP, None, ("ctx", "ep")),
        P(TP, ("ctx", "ep"), None),
        P("ctx", None),
        P("ctx", None),
    )
    out_specs = P("ctx", TP_EP)
    return jax.shard_map(
        on_device, mesh=torus, in_specs=in_specs, out_specs=out_specs, check_vma=False
    )
```

profile of v0, /device:TPU:1, one launch (start us, length us, event | category | flops | bytes accessed | tf_op | source)
XLA Modules:
  0.0 661.8 jit_solution(15073614211163878347)
XLA Ops:
  7.3 1.2 copy.45
  8.4 0.9 copy.47
  9.4 31.8 %all_gather.12 = bf16[2048,128]{1,0:T(8,128)(2,1)S(1)} all-gather(bf16[256,128]{1,0:T(8,128)(2,1)} %param.15), channel_id=1, replica_groups=mesh['ctx'=8,'tp_0'=4,'tp_1'=2,'ep'=2] {'ctx'}, dimensions={0}, use_global_device_ids=true | all-gather | bytes 589824 | tf_op jit(solution)/shard_map/all_gather | solution.py:75
  41.6 2.0 fusion.36
  43.6 30.6 %all_gather.13 = bf16[2048,128]{0,1:T(8,128)(2,1)S(1)} all-gather(bf16[256,128]{0,1:T(8,128)(2,1)S(1)} %copy.47), channel_id=1, replica_groups=mesh['ctx'=8,'tp_0'=4,'tp_1'=2,'ep'=2] {'ctx'}, dimensions={0}, use_global_device_ids=true | all-gather | bytes 589824 | tf_op jit(solution)/shard_map/all_gather | solution.py:76
  74.3 2.6 fusion.39
  76.9 2.9 fusion.55
  79.8 19.2 %all-gather.3.cloned.1.call-done = bf16[768,3072]{1,0:T(8,128)(2,1)} async-done(((bf16[768,384]{1,0:T(8,128)(2,1)}), bf16[768,3072]{1,0:T(8,128)(2,1)}) %all-gather.3.cloned.1.call-update) | async-done | bytes 4718608 | tf_op jit(solution)/shard_map/all_gather | solution.py:98
  99.0 3.8 convolution_convert_fusion
  102.8 1.3 copy.73
  104.1 5.7 all-to-all-start
  110.7 19.6 %all-to-all-done = bf16[8,256,384]{2,1,0:T(8,128)(2,1)S(1)} async-done(((bf16[8,256,384]{2,1,0:T(8,128)(2,1)}), bf16[8,256,384]{2,1,0:T(8,128)(2,1)S(1)}, u32[]{:S(2)}, u32[]{:S(2)}) %all-to-all-start) | async-done | bytes 1572896 | tf_op jit(solution)/shard_map/all_to_all | solution.py:21
  131.4 4.3 all-to-all-start.1
  135.7 5.8 all-to-all-done.1
  142.2 4.2 all_to_all.35
  146.4 12.7 %all_to_all.36 = bf16[4,2,1,1,96,384]{5,4,1,3,2,0:T(8,128)(2,1)} all-to-all(bf16[4,2,1,1,96,384]{5,4,1,3,2,0:T(8,128)(2,1)S(1)} %copy.51), channel_id=1, replica_groups=mesh['ctx'=8,'tp_0'=4,'tp_1'=2,'ep'=2] {'tp_0'}, dimensions={0} | all-to-all | bytes 1179648 | tf_op jit(solution)/shard_map/all_to_all | solution.py:45
  159.4 14.6 %reshape_squeeze.11 = bf16[512,8,2,384]{3,2,1,0:T(2,128)(2,1)} reshape(bf16[1,512,6144]{2,1,0:T(8,128)(2,1)} %param.21) | data formatting | bytes 12582912 | tf_op jit(solution)/shard_map/reshape;squeeze | solution.py:142
  174.0 15.4 %constant_dynamic-slice_fusion.3 = (bf16[512,8,1,384]{3,2,1,0:T(2,128)(2,1)}, bf16[512,8,1,384]{3,2,1,0:T(2,128)(2,1)S(1)}) fusion(bf16[512,8,2,384]{3,2,1,0:T(2,128)(2,1)} %reshape_squeeze.11, s32[]{:T(128)S(6)} %select_n.93, s32[]{:T(128)S(6)} %select_n.94), kind=kLoop, calls=%fused_computation.93 | loop fusion | bytes 12582920 | tf_op jit(solution)/shard_map/jit(dynamic_index_in_dim)/dynamic_slice | solution.py:144
  189.4 2.8 copy.71
  192.5 226.1 %all-gather.5.cloned.1.call-done = bf16[16,8,96,384]{3,2,1,0:T(8,128)(2,1)} async-done(((bf16[1,8,96,384]{3,2,1,0:T(8,128)(2,1)}), bf16[16,8,96,384]{3,2,1,0:T(8,128)(2,1)}) %all-gather.5.cloned.1.call-update) | async-done | bytes 9437200 | tf_op jit(solution)/shard_map/all_gather | solution.py:122
  419.0 88.4 %while.17 = (s32[]{:T(128)}, f32[8,96,512]{2,1,0:T(8,128)S(1)}, f32[8,96,512]{2,1,0:T(8,128)S(1)}, bf16[16,8,96,384]{3,2,1,0:T(8,128)(2,1)}, bf16[8,2,384,512]{3...) while((s32[]{:T(128)}, f32[8,96,512]{2,1,0:T(8,128)S(1)}, ...), condition=%wide.region_11.12_spmd, body=%wide.region_10.11_spmd.sunk | while | flops 604078080 | bytes 9045304 | solution.py:140
  419.1 2.7 fusion.102
  421.8 2.7 fusion.101
  424.6 2.7 fusion.102
  427.3 2.7 fusion.101
  430.1 2.7 fusion.102
  432.8 2.7 fusion.101
  435.6 2.7 fusion.102
  438.4 2.7 fusion.101
  441.2 2.7 fusion.102
  443.9 2.7 fusion.101
  446.7 2.7 fusion.102
  449.4 2.7 fusion.101
  452.2 2.7 fusion.102
  454.9 2.7 fusion.101
  457.7 2.7 fusion.102
  460.5 2.7 fusion.101
  463.3 2.7 fusion.102
  466.0 2.7 fusion.101
  468.8 2.7 fusion.102
  471.5 2.7 fusion.101
  474.3 2.7 fusion.102
  477.0 2.7 fusion.101
  479.8 2.7 fusion.102
  482.5 2.7 fusion.101
  485.3 2.7 fusion.102
  488.1 2.7 fusion.101
  490.9 2.7 fusion.102
  493.6 2.7 fusion.101
  496.4 2.7 fusion.102
  499.1 2.7 fusion.101
  501.9 2.7 fusion.102
  504.6 2.7 fusion.101
  507.8 7.8 %collective-permute-start = (bf16[8,96,512]{2,1,0:T(8,128)(2,1)S(1)}, bf16[8,96,512]{2,1,0:T(8,128)(2,1)S(1)}, u32[]{:S(2)}, u32[]{:S(2)}) collective-permute-start(bf16[8,96,512]{2,1,0:T(8,128)(2,1)S(1)} %multiply_convert_fusion), channel_id=1, source_target_pairs={{0,1},{1,0},{2,3},{3,2},{4,5},{5,4},{6,7},{7,6},{8,9},{9,8},{10,11... | collective-permute-start | bytes 2359304 | tf_op jit(solution)/shard_map/ppermute | solution.py:55
  515.6 3.9 copy.72
  519.5 13.0 %collective-permute-done = bf16[8,96,512]{2,1,0:T(8,128)(2,1)S(1)} collective-permute-done((bf16[8,96,512]{2,1,0:T(8,128)(2,1)S(1)}, bf16[8,96,512]{2,1,0:T(8,128)(2,1)S(1)}, u32[]{:S(2)}, u32[]{:S(2)}) %collective-permute-start) | collective-permute-done | bytes 786464 | tf_op jit(solution)/shard_map/ppermute | solution.py:55
  532.6 6.7 %fusion.48 = bf16[8,96,8,384]{3,1,2,0:T(8,128)(2,1)S(1)} fusion(bf16[512,8,384]{2,0,1:T(8,128)(2,1)} %collective-permute-done.1, bf16[512,8,384]{2,0,1:T(8,128)(2,1)S(1)} %bitcast.178, bf16[8,96,512]{2,1,0:T(8,128)(2,1)S(1)} %collective-permute-done, bf16[8,96,512]{2,1,0:T(8,128)(2,1)S(1)} %multiply_convert_fusion), kind=kOutput, calls=%fused_computation.40 | convolution fusion | flops 4849926144 | bytes 12582912 | tf_op jit(solution)/shard_map/csf,ftj->cstj/dot_general | solution.py:150
  539.2 1.9 copy.56
  541.1 3.3 copy.66
  544.5 91.3 %reduce-scatter.2.cloned.1.call-done = bf16[96,3072]{1,0:T(8,128)(2,1)} async-done(((bf16[768,3072]{1,0:T(8,128)(2,1)}), bf16[96,3072]{1,0:T(8,128)(2,1)}) %reduce-scatter.2.cloned.1.call-update) | async-done | bytes 589840 | tf_op jit(solution)/shard_map/reduce_scatter | solution.py:153
  635.7 1.1 copy.67
  637.8 6.2 all-to-all-start.4
  644.1 10.0 %all-to-all-done.4 = bf16[1,96,8,384]{3,1,0,2:T(8,128)(2,1)S(1)} async-done(((bf16[1,96,8,384]{3,1,0,2:T(8,128)(2,1)}), bf16[1,96,8,384]{3,1,0,2:T(8,128)(2,1)S(1)}, u32[]{:S(2)}, u32[]{:S(2)}) %all-to-all-start.4) | async-done | bytes 589856 | tf_op jit(solution)/shard_map/all_to_all | solution.py:160
  654.1 1.2 fusion.51
  (64 shorter events, 6.5 us)
Async XLA Ops:
  6.5 92.4 %all-gather.3.cloned.1.call-start = ((), (), s32[]{:S(2)}) async-start(), calls=%async_computation.6 | async-start | bytes 5308416 | tf_op jit(solution)/shard_map/all_gather | solution.py:98
  102.7 7.1 %copy-start.3 = (s32[256,2]{0,1:T(2,128)S(1)}, s32[256,2]{0,1:T(2,128)}, u32[]{:S(2)}) copy-start(s32[256,2]{0,1:T(2,128)} %param.22) | copy-start | bytes 6148
  102.7 27.8 %copy-start = (bf16[256,384]{1,0:T(8,128)(2,1)S(1)}, bf16[256,384]{1,0:T(8,128)(2,1)}, u32[]{:S(2)}) copy-start(bf16[256,384]{1,0:T(8,128)(2,1)} %param.13) | copy-start | bytes 589828
  102.7 33.0 %copy-start.5 = (bf16[384]{0:T(512)(128)(2,1)S(1)}, bf16[384]{0:T(512)(128)(2,1)}, u32[]{:S(2)}) copy-start(bf16[384]{0:T(512)(128)(2,1)} %param.18) | copy-start | bytes 2308
  104.1 26.3 %all-to-all-start = ((bf16[8,256,384]{2,1,0:T(8,128)(2,1)}), bf16[8,256,384]{2,1,0:T(8,128)(2,1)S(1)}, u32[]{:S(2)}, u32[]{:S(2)}) async-start(bf16[8,256,384]{2,1,0:T(8,128)(2,1)} %bitcast.152), calls=%async_computation | async-start | bytes 3145728 | tf_op jit(solution)/shard_map/all_to_all | solution.py:21
  130.7 43.3 %copy-start.1 = (bf16[256,384]{1,0:T(8,128)(2,1)}, bf16[256,384]{1,0:T(8,128)(2,1)S(1)}, u32[]{:S(2)}) copy-start(bf16[256,384]{1,0:T(8,128)(2,1)S(1)} %get-tuple-element.198) | copy-start | bytes 589828
  131.4 10.2 %all-to-all-start.1 = ((f32[16,256,1]{1,2,0:T(1,128)}), f32[16,256,1]{1,2,0:T(1,128)S(1)}, u32[]{:S(2)}, u32[]{:S(2)}) async-start(f32[16,256,1]{1,2,0:T(1,128)} %broadcast_in_dim.96), calls=%async_computation.1 | async-start | bytes 32768 | tf_op jit(solution)/shard_map/all_to_all | solution.py:27
  135.7 282.9 %all-gather.5.cloned.1.call-start = ((), (), s32[]{:S(2)}) async-start(), calls=%async_computation.7 | async-start | bytes 10027008 | tf_op jit(solution)/shard_map/all_gather | solution.py:122
  159.2 476.6 %reduce-scatter.2.cloned.1.call-start = ((), (), s32[]{:S(2)}) async-start(), calls=%async_computation.8 | async-start | bytes 5308416 | tf_op jit(solution)/shard_map/reduce_scatter | solution.py:153
  192.2 327.3 %collective-permute-start.1 = (bf16[512,8,384]{2,0,1:T(8,128)(2,1)}, bf16[512,8,384]{2,0,1:T(8,128)(2,1)}, u32[]{:S(2)}, u32[]{:S(2)}) collective-permute-start(bf16[512,8,384]{2,0,1:T(8,128)(2,1)} %bitcast.149), channel_id=1, source_target_pairs={{0,1},{1,0},{2,3},{3,2},{4,5},{5,4},{6,7},{7,6},{8,9},{9,8},{10,11... | collective-permute-start | bytes 9437192 | tf_op jit(solution)/shard_map/ppermute | solution.py:55
  507.8 24.7 %collective-permute-start = (bf16[8,96,512]{2,1,0:T(8,128)(2,1)S(1)}, bf16[8,96,512]{2,1,0:T(8,128)(2,1)S(1)}, u32[]{:S(2)}, u32[]{:S(2)}) collective-permute-start(bf16[8,96,512]{2,1,0:T(8,128)(2,1)S(1)} %multiply_convert_fusion), channel_id=1, source_target_pairs={{0,1},{1,0},{2,3},{3,2},{4,5},{5,4},{6,7},{7,6},{8,9},{9,8},{10,11... | collective-permute-start | bytes 2359304 | tf_op jit(solution)/shard_map/ppermute | solution.py:55
  544.4 99.6 %copy-start.4 = (s32[256,2]{0,1:T(2,128)S(1)}, s32[256,2]{0,1:T(2,128)}, u32[]{:S(2)}) copy-start(s32[256,2]{0,1:T(2,128)} %param.23) | copy-start | bytes 6148
  544.4 109.6 %copy-start.2 = (bf16[256,384]{1,0:T(8,128)(2,1)S(1)}, bf16[256,384]{1,0:T(8,128)(2,1)}, u32[]{:S(2)}) copy-start(bf16[256,384]{1,0:T(8,128)(2,1)} %copy-done.1) | copy-start | bytes 589828
  637.8 16.3 %all-to-all-start.4 = ((bf16[1,96,8,384]{3,1,0,2:T(8,128)(2,1)}), bf16[1,96,8,384]{3,1,0,2:T(8,128)(2,1)S(1)}, u32[]{:S(2)}, u32[]{:S(2)}) async-start(bf16[1,96,8,384]{3,1,0,2:T(8,128)(2,1)} %copy.57), calls=%async_computation.5 | async-start | bytes 1179648 | tf_op jit(solution)/shard_map/all_to_all | solution.py:160
Sparse Core Ops, SparseCore 0:
  9.5 89.3 all-gather.2
  159.3 259.2 all-gather.4
  544.6 91.1 reduce-scatter.1
where the time goes:
time: 663 us; the launch traced here: 662 us
  waiting for transfers between devices  386 us (58%)
  matrix products  104 us (16%)
  blocking collectives  79.4 us (12%)
  local copies, waits for them, and re-layouts  49.3 us (7%)
  starting transfers between devices  24.5 us (4%)
  between operations  13.4 us (2%)
    all_gather x1, waiting for transfers between devices, on_device(): piece = lax.all_gather(arrived, ('ctx', 'ep'), axis=0, tiled=True)  226 us
    reduce_scatter x1, waiting for transfers between devices, on_device(): lax.psum_scatter(product.reshape(blocks * capacity, tp_size * feat_dev).a...  91.3 us
    dot_general x16, matrix products, one_row(): jnp.einsum('tsj,tjf->sf', row, gate_part, preferred_element_type=jnp.floa...  43.6 us
    dot_general x16, matrix products, one_row(): jnp.einsum('tsj,tjf->sf', row, up_part, preferred_element_type=jnp.float32)  43.5 us
    all_gather x1, blocking collectives, on_device(): key_piece = lax.all_gather(keys, 'ctx', axis=0, tiled=True)  31.8 us
    all_gather x1, blocking collectives, on_device(): value_piece = lax.all_gather(values, 'ctx', axis=0, tiled=True)  30.6 us
    all_to_all x1, waiting for transfers between devices, sent_and_summed(): lax.all_to_all(tiles, axis, split_axis=0, concat_axis=0, tiled=True)  19.6 us
    all_gather x1, waiting for transfers between devices, on_device(): lax.all_gather(w_out, 'ctx', axis=1, tiled=True)  19.2 us
  transfers between devices with their start and end apart: 8, of which 7 were waited for; matrix products, arithmetic and copies ran while one was open for 21% of the time, Pallas kernels for 0%

commit v1 on v0

v1 whole, which is shorter than its diff:
```python
import jax
import jax.numpy as jnp
from jax import lax
from jax.experimental import pallas as pl
from jax.experimental.pallas import tpu as pltpu
from jax.sharding import Mesh
from jax.sharding import PartitionSpec as P

D = 6144
HD = 128
CTX = ("zh", "x")
TP = ("y", "core")
TP_EP = ("y", "core", "zl")
MESH_ID = pl.DeviceIdType.MESH
F32 = jnp.float32
BF16 = jnp.bfloat16
FAR_FIRST = (2, 1, -1, 0)


def wrapped(index, size=4):
    return lax.rem(index + size, size)


class Place:
    def __init__(self):
        self.x = lax.axis_index("x")
        self.z = lax.axis_index("zh") * 2 + lax.axis_index("zl")
        self.y = lax.axis_index("y")
        self.core = lax.axis_index("core")
        self.tp = self.y * 2 + self.core

    def beside(self, axis, step):
        if axis == "x":
            return {"x": wrapped(self.x + step)}
        z = wrapped(self.z + step)
        return {"zh": z // 2, "zl": lax.rem(z, 2)}

    def tp_peer(self, step):
        other = lax.rem(self.tp + step, 8)
        return {"y": other // 2, "core": lax.rem(other, 2)}

    def greet(self, tp_peers):
        barrier = pltpu.get_barrier_semaphore()
        peers = [self.beside(axis, step) for axis in ("x", "z") for step in (1, -1)]
        if tp_peers:
            peers += [self.tp_peer(step) for step in range(1, 8)]
        for peer in peers:
            pl.semaphore_signal(barrier, inc=1, device_id=peer, device_id_type=MESH_ID)
        pl.semaphore_wait(barrier, len(peers))


class Link:
    def __init__(self, send_sem, recv_sem):
        self.send_sem, self.recv_sem, self.open = send_sem, recv_sem, []

    def copy(self, number, src, dst, device):
        return pltpu.make_async_remote_copy(
            src_ref=src,
            dst_ref=dst,
            send_sem=self.send_sem.at[number],
            recv_sem=self.recv_sem.at[number],
            device_id=device,
            device_id_type=MESH_ID,
        )

    def send(self, number, src, dst, device):
        copy = self.copy(number, src, dst, device)
        copy.start()
        self.open.append(copy)

    def arrived(self, number, dst, device):
        self.copy(number, dst, dst, device).wait_recv()

    def finish(self):
        for copy in self.open:
            copy.wait_send()
        self.open = []


GATHER_COPIES = 40


def plane_gather(place, link, piece, first=0):
    here = (place.x, place.z)

    def block(part, along_f, along_s, half=None):
        f, s = (here[0], here[1]) if part == 0 else (here[1], here[0])
        f, s = wrapped(f + along_f), wrapped(s + along_s)
        return piece(f, s, part, half) if part == 0 else piece(s, f, part, half)

    def f_axis(part):
        return "xz"[part]

    def s_axis(part):
        return "zx"[part]

    def number(part, kind, g, direction):
        base = {"near": 0, "far": 2, "near2": 4, "far2": 12}[kind]
        return first + part * 20 + base + (FAR_FIRST.index(g) * 2 if kind in ("near2", "far2") else 0) + direction

    def pass_on(part, g):
        ref = block(part, g, 0)
        for direction, step in ((0, 1), (1, -1)):
            link.send(number(part, "near2", g, direction), ref, ref, place.beside(s_axis(part), step))

    for part in (0, 1):
        ref = block(part, 0, 0)
        for direction, step in ((0, 1), (1, -1)):
            link.send(number(part, "near", 0, direction), ref, ref, place.beside(f_axis(part), step))
    for part in (0, 1):
        pass_on(part, 0)
    for part in (0, 1):
        for direction, step in ((0, 1), (1, -1)):
            back = place.beside(f_axis(part), -step)
            link.arrived(number(part, "near", 0, direction), block(part, -step, 0), back)
            ref = block(part, -step, 0, direction)
            link.send(number(part, "far", 0, direction), ref, ref, place.beside(f_axis(part), step))
    for part in (0, 1):
        pass_on(part, -1)
        pass_on(part, 1)

    def relay(part, g):
        for direction, step in ((0, 1), (1, -1)):
            back = place.beside(s_axis(part), -step)
            link.arrived(number(part, "near2", g, direction), block(part, g, -step), back)
            ref = block(part, g, -step, direction)
            link.send(number(part, "far2", g, direction), ref, ref, place.beside(s_axis(part), step))

    for part in (0, 1):
        relay(part, 0)
    for part in (0, 1):
        for direction, step in ((0, 1), (1, -1)):
            back = place.beside(f_axis(part), -step)
            link.arrived(number(part, "far", 0, direction), block(part, 2, 0, direction), back)
        pass_on(part, 2)
    for g in (-1, 1, 2):
        for part in (0, 1):
            relay(part, g)
    for g in (0, -1, 1, 2):
        for part in (0, 1):
            for direction, step in ((0, 1), (1, -1)):
                back = place.beside(s_axis(part), -step)
                link.arrived(number(part, "far2", g, direction), block(part, g, 2, direction), back)


def experts_kernel(
    slots,
    w_gate,
    w_up,
    w_down,
    out,
    rows,
    gate_w,
    up_w,
    down_w,
    gate_acc,
    up_acc,
    hidden,
    partial,
    got_half,
    got_part,
    result,
    returned,
    load_sem,
    send_sem,
    recv_sem,
):
    place = Place()
    link = Link(send_sem, recv_sem)
    loads = [
        pltpu.make_async_copy(src, dst, load_sem.at[i])
        for i, (src, dst) in enumerate(((w_gate, gate_w), (w_up, up_w), (w_down, down_w)))
    ]
    for load in loads:
        load.start()
    place.greet(True)

    base = 80
    for step in range(1, 8):
        target = lax.rem(place.tp + step, 8)
        link.send(base + step, slots.at[target], rows.at[place.x, place.z, place.tp], place.tp_peer(step))
    rows[place.x, place.z, place.tp] = slots[place.tp]
    for step in range(1, 8):
        source = lax.rem(place.tp + 8 - step, 8)
        link.arrived(base + step, rows.at[place.x, place.z, source], place.tp_peer(8 - step))

    def block_of_rows(x, z, part, half):
        if half is None:
            return rows.at[x, z, pl.ds(part * 4, 4)]
        return rows.at[x, z, pl.ds(part * 4 + half * 2, 2)]

    plane_gather(place, link, block_of_rows)

    loads[0].wait()
    loads[1].wait()
    for zh in range(2):
        gate_acc[...] = jnp.zeros_like(gate_acc)
        up_acc[...] = jnp.zeros_like(up_acc)

        @pl.loop(0, 8)
        def _(t):
            even = rows[:, 2 * zh, t].reshape(384, 384)
            odd = rows[:, 2 * zh + 1, t].reshape(384, 384)
            left = jnp.concatenate([even, odd], axis=1)
            span = pl.ds(pl.multiple_of(t * 768, 768), 768)
            gate_acc[...] += jnp.dot(left, gate_w[span, :], preferred_element_type=F32)
            up_acc[...] += jnp.dot(left, up_w[span, :], preferred_element_type=F32)

        gate = gate_acc[...]
        value = gate / (1.0 + jnp.exp(-gate)) * up_acc[...]
        hidden[pl.ds(zh * 4, 4)] = value.astype(BF16).reshape(4, 96, 512)
    loads[2].wait()

    def compute(part, g):
        if part == 0:
            x = wrapped(place.x + g)
            left = jnp.concatenate([hidden[x], hidden[4 + x]], axis=0)

            @pl.loop(0, 4)
            def _(t):
                right = down_w[:, pl.ds(pl.multiple_of(t * 768, 768), 768)]
                both = jnp.dot(left, right, preferred_element_type=F32).astype(BF16)
                for zh in range(2):
                    for e in range(2):
                        partial[x, zh * 2 + e, t] = both[zh * 96 : zh * 96 + 96, e * 384 : e * 384 + 384]
        else:
            z = wrapped(place.z + g)
            left = hidden[pl.ds((z // 2) * 4, 4)].reshape(384, 512)

            @pl.loop(4, 8)
            def _(t):
                start = (2 * t + lax.rem(z, 2)) * 384
                right = down_w[:, pl.ds(pl.multiple_of(start, 384), 384)]
                both = jnp.dot(left, right, preferred_element_type=F32).astype(BF16)
                partial[:, z, t] = both.reshape(4, 96, 384)

    def block(part, along_f, along_s):
        x, z = (along_f, along_s) if part == 0 else (along_s, along_f)
        return wrapped(place.x + x), wrapped(place.z + z)

    def half_of(where, part, half):
        return partial.at[where[0], where[1], pl.ds(part * 4 + half * 2, 2)]

    def part_of(where, part):
        return partial.at[where[0], where[1], pl.ds(part * 4, 4)]

    def add(target, *sources):
        total = target[...].astype(F32)
        for source in sources:
            total = total + source[...].astype(F32)
        target[...] = total.astype(BF16)

    class Ring:
        def __init__(self, part, stage, axis, at):
            self.part, self.stage, self.axis, self.at = part, stage, axis, at
            self.number = 100 + (part * 5 + stage) * 4

        def far(self):
            for direction, step in ((0, 1), (1, -1)):
                link.send(
                    self.number + direction,
                    half_of(self.at(2), self.part, direction),
                    got_half.at[self.part, self.stage, direction],
                    place.beside(self.axis, step),
                )

        def near(self):
            for direction, step in ((0, 1), (1, -1)):
                got = got_half.at[self.part, self.stage, direction]
                link.arrived(self.number + direction, got, place.beside(self.axis, -step))
                add(half_of(self.at(step), self.part, direction), got)
                link.send(
                    self.number + 2 + direction,
                    part_of(self.at(step), self.part),
                    got_part.at[self.part, self.stage, direction],
                    place.beside(self.axis, step),
                )

        def receive(self):
            gots = []
            for direction, step in ((0, 1), (1, -1)):
                got = got_part.at[self.part, self.stage, direction]
                link.arrived(self.number + 2 + direction, got, place.beside(self.axis, -step))
                gots.append(got)
            return gots

        def end(self):
            add(part_of(self.at(0), self.part), *self.receive())

    outer = [
        {
            g: Ring(part, FAR_FIRST.index(g), "zx"[part], lambda step, part=part, g=g: block(part, g, step))
            for g in FAR_FIRST
        }
        for part in (0, 1)
    ]
    inner = [Ring(part, 4, "xz"[part], lambda step, part=part: block(part, step, 0)) for part in (0, 1)]
    for g in FAR_FIRST:
        for part in (0, 1):
            compute(part, g)
            outer[part][g].far()
    for g in FAR_FIRST:
        for part in (0, 1):
            outer[part][g].near()
    for part in (0, 1):
        outer[part][2].end()
        inner[part].far()
    for part in (0, 1):
        outer[part][1].end()
        outer[part][-1].end()
        inner[part].near()
    base = 88
    for part in (0, 1):
        outer[part][0].end()
        gots = inner[part].receive()
        total = part_of(inner[part].at(0), part)[...].astype(F32)
        for got in gots:
            total = total + got[...].astype(F32)
        result[pl.ds(part * 4, 4)] = total.astype(BF16)
    for step in range(1, 8):
        target = lax.rem(place.tp + step, 8)
        link.send(base + step, result.at[target], returned.at[place.tp], place.tp_peer(step))
    returned[place.tp] = result[place.tp]
    for step in range(1, 8):
        source = lax.rem(place.tp + 8 - step, 8)
        link.arrived(base + step, returned.at[source], place.tp_peer(8 - step))
    link.finish()
    out[...] = returned[...]


def experts(slots, w_gate, w_up, w_down):
    copies = 140
    return pl.pallas_call(
        experts_kernel,
        out_shape=jax.ShapeDtypeStruct((8, 96, 384), BF16),
        in_specs=[pl.BlockSpec(memory_space=pltpu.VMEM)] + [pl.BlockSpec(memory_space=pl.ANY)] * 3,
        out_specs=pl.BlockSpec(memory_space=pltpu.VMEM),
        scratch_shapes=[
            pltpu.VMEM((4, 4, 8, 96, 384), BF16),
            pltpu.VMEM((6144, 512), BF16),
            pltpu.VMEM((6144, 512), BF16),
            pltpu.VMEM((512, 6144), BF16),
            pltpu.VMEM((384, 512), F32),
            pltpu.VMEM((384, 512), F32),
            pltpu.VMEM((8, 96, 512), BF16),
            pltpu.VMEM((4, 4, 8, 96, 384), BF16),
            pltpu.VMEM((2, 5, 2, 2, 96, 384), BF16),
            pltpu.VMEM((2, 5, 2, 4, 96, 384), BF16),
            pltpu.VMEM((8, 96, 384), BF16),
            pltpu.VMEM((8, 96, 384), BF16),
            pltpu.SemaphoreType.DMA((3,)),
            pltpu.SemaphoreType.DMA((copies,)),
            pltpu.SemaphoreType.DMA((copies,)),
        ],
        compiler_params=pltpu.CompilerParams(
            collective_id=1, has_side_effects=True, vmem_limit_bytes=64 * 1024 * 1024 - 128 * 1024
        ),
        name="experts",
    )(slots, w_gate, w_up, w_down)


def split_up(x, dim, size):
    dims = x.shape
    tiles = x.reshape(*dims[:dim], size, dims[dim] // size, *dims[dim + 1 :])
    return jnp.moveaxis(tiles, dim, 0)


def sent_and_summed(x, axis, dim):
    tiles = split_up(x, dim, lax.axis_size(axis))
    arrived = lax.all_to_all(tiles, axis, split_axis=0, concat_axis=0, tiled=True)
    return arrived.astype(jnp.float32).sum(axis=0)


def from_everyone(x, axis):
    size = lax.axis_size(axis)
    return lax.all_to_all(jnp.broadcast_to(x[None], (size, *x.shape)), axis, 0, 0, tiled=True)


def taken_together(x, axis):
    everything = from_everyone(x, axis)
    return jnp.sum(everything, axis=0)


def on_device(
    resid, queries, keys, values, w_out, norm_gain, w_gate, w_up, w_down, expert_ids, route_units
):
    tp_size = lax.axis_size(TP)
    tok_rows = queries.shape[0]
    heads_dev = queries.shape[1] // HD
    kv_dev = keys.shape[1] // HD
    group = heads_dev // kv_dev
    feat_dev = resid.shape[1]
    capacity = 3 * tok_rows // tp_size
    first_pos = lax.axis_index(CTX) * tok_rows
    query_heads = queries.reshape(tok_rows, kv_dev, group, HD)
    query_pos = first_pos + jnp.arange(tok_rows, dtype=jnp.int32)
    running_max = jnp.full((kv_dev, group, tok_rows), -1e30, jnp.float32)
    key_piece = lax.all_gather(keys, CTX, axis=0, tiled=True)
    value_piece = lax.all_gather(values, CTX, axis=0, tiled=True)
    count = key_piece.shape[0]
    key_rows = key_piece.reshape(count, kv_dev, HD)
    value_rows = value_piece.reshape(count, kv_dev, HD)
    scores = jnp.einsum(
        "tkgd,nkd->kgtn", query_heads, key_rows, preferred_element_type=jnp.float32
    ) * HD ** (-0.5)
    key_pos = jnp.arange(count, dtype=jnp.int32)
    allowed = (key_pos[None, :] <= query_pos[:, None])[None, None]
    block_max = jnp.max(jnp.where(allowed, scores, -1e30), axis=-1)
    new_max = jnp.maximum(running_max, block_max)
    probs = jnp.where(allowed, jnp.exp(scores - new_max[..., None]), 0.0)
    new_sum = jnp.sum(probs, axis=-1)
    probs_b = probs.astype(jnp.bfloat16)
    update = jnp.einsum("kgtn,nkd->kgtd", probs_b, value_rows, preferred_element_type=jnp.float32)
    attn = (
        (update / new_sum[..., None])
        .transpose(2, 0, 1, 3)
        .reshape(tok_rows, heads_dev * HD)
        .astype(jnp.bfloat16)
    )
    partial_proj = jnp.dot(
        attn, lax.all_gather(w_out, CTX, axis=1, tiled=True), preferred_element_type=jnp.float32
    )
    proj = sent_and_summed(partial_proj.astype(jnp.bfloat16), TP, 1)
    hres = (resid.astype(jnp.float32) + proj).astype(jnp.bfloat16)
    hfloat = hres.astype(jnp.float32)
    square_total = taken_together(jnp.sum(hfloat * hfloat, axis=1, keepdims=True), TP_EP)
    normed = (hfloat * lax.rsqrt(square_total / D + 1e-05) * norm_gain.astype(jnp.float32)).astype(
        jnp.bfloat16
    )
    onehot = (expert_ids[..., None] == jnp.arange(tp_size, dtype=jnp.int32)).astype(jnp.int32)
    per_token = jnp.sum(onehot, axis=1)
    earlier = jnp.cumsum(per_token, axis=0) - per_token
    slot = jnp.sum(onehot * earlier[:, None, :], axis=-1)
    codes = expert_ids * capacity + slot
    slot_ids = jnp.arange(tp_size * capacity, dtype=jnp.int32)
    picks = (
        (slot_ids[:, None] == codes[None, :, 0]) | (slot_ids[:, None] == codes[None, :, 1])
    ).astype(jnp.bfloat16)
    dispatched = jnp.dot(picks, normed, preferred_element_type=jnp.float32).astype(jnp.bfloat16)
    returned = experts(dispatched.reshape(tp_size, capacity, feat_dev), w_gate[0], w_up[0], w_down[0])
    units = route_units.astype(jnp.float32)
    weights = (units / jnp.sum(units, axis=-1, keepdims=True)).astype(jnp.bfloat16)
    combine = jnp.where(slot_ids[None, :] == codes[:, 0:1], weights[:, 0:1], 0.0) + jnp.where(
        slot_ids[None, :] == codes[:, 1:2], weights[:, 1:2], 0.0
    )
    moe = jnp.dot(
        combine, returned.reshape(tp_size * capacity, feat_dev), preferred_element_type=jnp.float32
    )
    return (hfloat + moe).astype(jnp.bfloat16)


def solution(mesh):
    torus = Mesh(mesh.devices.reshape(2, 4, 4, 2, 2), ("zh", "x", "y", "core", "zl"))
    in_specs = (
        P(CTX, TP_EP),
        P(CTX, TP),
        P(CTX, TP),
        P(CTX, TP),
        P(TP, ("zh", "x", "zl")),
        P(TP_EP),
        P(TP, None, ("zh", "x", "zl")),
        P(TP, None, ("zh", "x", "zl")),
        P(TP, ("zh", "x", "zl"), None),
        P(CTX, None),
        P(CTX, None),
    )
    return jax.shard_map(
        on_device, mesh=torus, in_specs=in_specs, out_specs=P(CTX, TP_EP), check_vma=False
    )
```

time: 663 us -> 297 us (0.45)
  waiting for transfers between devices: 386 us -> 45.3 us
  Pallas kernels: 0 us -> 143 us
  matrix products: 104 us -> 13.2 us
  local copies, waits for them, and re-layouts: 49.3 us -> 4.31 us
  blocking collectives: 79.4 us -> 62.5 us
  starting transfers between devices: 24.5 us -> 9.95 us
    all_gather x2 -> x1, waiting for transfers between devices: 245 us -> 19.2 us  [on_device(): lax.all_gather(w_out, CTX, axis=1, tiled=True)]
    pallas_call x0 -> x1, Pallas kernels: none -> 143 us  [experts(): pl.pallas_call(experts_kernel, out_shape=jax.ShapeDtypeStruct((8, 96, 384...]
    dot_general x34 -> x1, matrix products: 97.5 us -> 3.75 us  [on_device(): jnp.dot(attn, lax.all_gather(w_out, CTX, axis=1, tiled=True), preferred_e...]
    reduce_scatter x1 -> x0, waiting for transfers between devices: 91.3 us -> none  [on_device(): lax.psum_scatter(product.reshape(blocks * capacity, tp_size * feat_dev).a...]
    all_to_all x2 -> x0, blocking collectives: 16.9 us -> none  [moved_by_axis(): lax.all_to_all(tiles, axes[k], split_axis=k, concat_axis=k, tiled=True)]
    dynamic_slice x17 -> x0, local copies, waits for them, and re-layouts: 16 us -> none  [the longest x1 15.4 us: on_device(): mine_cols = lax.dynamic_index_in_dim(down_w, parity, 2, keepdims=False)]
    another operation x3 -> x1, local copies, waits for them, and re-layouts: 14.7 us -> 0.01 us  [the longest x1 14.6 us: on_device(): down_w = w_down[0].reshape(hidden_dev, tp_size, ep_size, feat_dev)]
    ppermute x2 -> x0, waiting for transfers between devices: 13 us -> none  [from_partner(): lax.ppermute(x, axis, [(i, i ^ 1 << distance) for i in range(lax.axis_siz...]
  transfers between devices with their start and end apart: 8 -> 3, of which waited for: 7 -> 3; matrix products, arithmetic and copies ran while one was open for 21% -> 4% of each run, Pallas kernels for 0% -> 0%
where the time goes in v1:
time: 297 us; the launch traced here: 296 us
  Pallas kernels  143 us (48%)
  blocking collectives  62.5 us (21%)
  waiting for transfers between devices  45.3 us (15%)
  between operations  13.6 us (5%)
  matrix products  13.2 us (4%)
  starting transfers between devices  9.95 us (3%)
  other arithmetic  4.69 us (2%)
  local copies, waits for them, and re-layouts  4.31 us (1%)
    pallas_call x1, Pallas kernels, experts(): pl.pallas_call(experts_kernel, out_shape=jax.ShapeDtypeStruct((8, 96, 384...  143 us
    all_gather x1, blocking collectives, on_device(): key_piece = lax.all_gather(keys, CTX, axis=0, tiled=True)  31.8 us
    all_gather x1, blocking collectives, on_device(): value_piece = lax.all_gather(values, CTX, axis=0, tiled=True)  30.6 us
    all_to_all x1, waiting for transfers between devices, sent_and_summed(): lax.all_to_all(tiles, axis, split_axis=0, concat_axis=0, tiled=True)  19.6 us
    all_gather x1, waiting for transfers between devices, on_device(): lax.all_gather(w_out, CTX, axis=1, tiled=True)  19.2 us
  transfers between devices with their start and end apart: 3, of which 3 were waited for; matrix products, arithmetic and copies ran while one was open for 4% of the time, Pallas kernels for 0%

profile of v1, /device:TPU:1, one launch (start us, length us, event | category | flops | bytes accessed | tf_op | source)
XLA Modules:
  0.0 296.2 jit_solution(5250277516044519605)
XLA Ops:
  6.5 0.0 all-gather.2.cloned.1.call-start
  6.5 0.7 all-gather.2.cloned.1.call-update
  7.3 1.2 copy.29
  8.4 0.9 copy.31
  9.4 31.8 %all_gather.9 = bf16[2048,128]{1,0:T(8,128)(2,1)S(1)} all-gather(bf16[256,128]{1,0:T(8,128)(2,1)} %param.13), channel_id=1, replica_groups=mesh['zh'=2,'x'=4,'y'=4,'core'=2,'zl'=2] {'zh','x'}, dimensions={0}, use_global_device_ids=true | all-gather | bytes 589824 | tf_op jit(solution)/shard_map/all_gather | solution.py:398
  41.2 0.3 iota_compare_fusion
  41.6 2.0 fusion
  43.6 30.6 %all_gather.10 = bf16[2048,128]{0,1:T(8,128)(2,1)S(1)} all-gather(bf16[256,128]{0,1:T(8,128)(2,1)S(1)} %copy.31), channel_id=1, replica_groups=mesh['zh'=2,'x'=4,'y'=4,'core'=2,'zl'=2] {'zh','x'}, dimensions={0}, use_global_device_ids=true | all-gather | bytes 589824 | tf_op jit(solution)/shard_map/all_gather | solution.py:399
  74.3 2.6 fusion.3
  76.9 2.9 fusion.13
  79.8 0.0 copy-start.1
  79.8 0.0 copy-start.2
  79.8 0.0 copy-start
  79.8 0.0 copy-start.3
  79.8 19.2 %all-gather.2.cloned.1.call-done = bf16[768,3072]{1,0:T(8,128)(2,1)} async-done(((bf16[768,384]{1,0:T(8,128)(2,1)}), bf16[768,3072]{1,0:T(8,128)(2,1)}) %all-gather.2.cloned.1.call-update) | async-done | bytes 4718608 | tf_op jit(solution)/shard_map/all_gather | solution.py:421
  99.0 3.8 %convolution_convert_fusion = bf16[256,3072]{1,0:T(8,128)(2,1)S(1)} fusion(bf16[256,768]{0,1:T(8,128)(2,1)S(1)} %bitcast.73, bf16[768,3072]{1,0:T(8,128)(2,1)} %all-gather.2.cloned.1.call-done), kind=kOutput, calls=%fused_computation.10 | convolution fusion | flops 1208745984 | bytes 6684672 | tf_op jit(solution)/shard_map/dot_general | solution.py:420
  102.7 1.3 copy.38
  104.1 5.7 %all-to-all-start = ((bf16[8,256,384]{2,1,0:T(8,128)(2,1)}), bf16[8,256,384]{2,1,0:T(8,128)(2,1)S(1)}, u32[]{:S(2)}, u32[]{:S(2)}) async-start(bf16[8,256,384]{2,1,0:T(8,128)(2,1)} %bitcast.67), calls=%async_computation | async-start | bytes 3145728 | tf_op jit(solution)/shard_map/all_to_all | solution.py:370
  109.7 0.0 copy-done.1
  109.7 0.6 reduce-window.6
  110.3 0.2 slice_reduce_fusion
  110.6 0.0 copy-done.2
  110.6 0.1 bitcast_subtract_fusion.1
  110.7 19.6 %all-to-all-done = bf16[8,256,384]{2,1,0:T(8,128)(2,1)S(1)} async-done(((bf16[8,256,384]{2,1,0:T(8,128)(2,1)}), bf16[8,256,384]{2,1,0:T(8,128)(2,1)S(1)}, u32[]{:S(2)}, u32[]{:S(2)}) %all-to-all-start) | async-done | bytes 1572896 | tf_op jit(solution)/shard_map/all_to_all | solution.py:370
  130.3 0.2 convert_reduce_fusion
  130.5 0.0 copy-done
  130.5 0.7 fusion.23
  131.3 0.6 broadcast_in_dim.71
  131.9 4.3 %all-to-all-start.1 = ((f32[16,256,1]{1,2,0:T(1,128)}), f32[16,256,1]{1,2,0:T(1,128)S(1)}, u32[]{:S(2)}, u32[]{:S(2)}) async-start(f32[16,256,1]{1,2,0:T(1,128)} %broadcast_in_dim.71), calls=%async_computation.1 | async-start | bytes 32768 | tf_op jit(solution)/shard_map/all_to_all | solution.py:376
  136.2 0.0 copy-done.3
  136.2 5.9 %all-to-all-done.1 = f32[16,256,1]{1,2,0:T(1,128)S(1)} async-done(((f32[16,256,1]{1,2,0:T(1,128)}), f32[16,256,1]{1,2,0:T(1,128)S(1)}, u32[]{:S(2)}, u32[]{:S(2)}) %all-to-all-start.1) | async-done | bytes 16416 | tf_op jit(solution)/shard_map/all_to_all | solution.py:376
  142.1 2.2 convolution_convert_fusion.1
  144.3 142.8 %experts.1 = bf16[8,96,384]{2,1,0:T(8,128)(2,1)} custom-call(bf16[8,96,384]{2,1,0:T(8,128)(2,1)} %bitcast.75, bf16[6144,512]{1,0:T(8,128)(2,1)} %bitcast.68, bf16[6144,512]{1,0:T(8,128)(2,1)} %bitcast.69, bf16[512,6144]{1,0:T(8,128)(2,1)} %bitcast.70), custom_call_target="tpu_custom_call" | custom-call | tf_op jit(solution)/shard_map/experts/pallas_call | solution.py:333
  287.1 2.3 fusion.9
  (14 shorter events, 0.2 us)
Async XLA Ops:
  6.5 92.4 %all-gather.2.cloned.1.call-start = ((), (), s32[]{:S(2)}) async-start(), calls=%async_computation.2 | async-start | bytes 5308416 | tf_op jit(solution)/shard_map/all_gather | solution.py:421
  79.8 30.0 %copy-start.1 = (s32[256,2]{0,1:T(2,128)S(1)}, s32[256,2]{0,1:T(2,128)}, u32[]{:S(2)}) copy-start(s32[256,2]{0,1:T(2,128)} %param.20) | copy-start | bytes 6148
  79.8 30.8 %copy-start.2 = (s32[256,2]{0,1:T(2,128)S(1)}, s32[256,2]{0,1:T(2,128)}, u32[]{:S(2)}) copy-start(s32[256,2]{0,1:T(2,128)} %param.21) | copy-start | bytes 6148
  79.8 50.8 %copy-start = (bf16[256,384]{1,0:T(8,128)(2,1)S(1)}, bf16[256,384]{1,0:T(8,128)(2,1)}, u32[]{:S(2)}) copy-start(bf16[256,384]{1,0:T(8,128)(2,1)} %param.11) | copy-start | bytes 589828
  79.8 56.4 %copy-start.3 = (bf16[384]{0:T(512)(128)(2,1)S(1)}, bf16[384]{0:T(512)(128)(2,1)}, u32[]{:S(2)}) copy-start(bf16[384]{0:T(512)(128)(2,1)} %param.16) | copy-start | bytes 2308
  104.1 26.3 %all-to-all-start = ((bf16[8,256,384]{2,1,0:T(8,128)(2,1)}), bf16[8,256,384]{2,1,0:T(8,128)(2,1)S(1)}, u32[]{:S(2)}, u32[]{:S(2)}) async-start(bf16[8,256,384]{2,1,0:T(8,128)(2,1)} %bitcast.67), calls=%async_computation | async-start | bytes 3145728 | tf_op jit(solution)/shard_map/all_to_all | solution.py:370
  131.9 10.2 %all-to-all-start.1 = ((f32[16,256,1]{1,2,0:T(1,128)}), f32[16,256,1]{1,2,0:T(1,128)S(1)}, u32[]{:S(2)}, u32[]{:S(2)}) async-start(f32[16,256,1]{1,2,0:T(1,128)} %broadcast_in_dim.71), calls=%async_computation.1 | async-start | bytes 32768 | tf_op jit(solution)/shard_map/all_to_all | solution.py:376
Sparse Core Ops, SparseCore 0:
  9.5 89.3 all-gather.1

commit v2 on v1

--- a/solution.py
+++ b/solution.py
@@ -27,7 +27,10 @@
         self.z = lax.axis_index("zh") * 2 + lax.axis_index("zl")
         self.y = lax.axis_index("y")
         self.core = lax.axis_index("core")
+        self.zl = lax.axis_index("zl")
         self.tp = self.y * 2 + self.core
+        self.ctx = lax.axis_index("zh") * 4 + self.x
+        self.member = self.tp * 2 + self.zl
 
     def beside(self, axis, step):
         if axis == "x":
@@ -39,32 +42,41 @@
         other = lax.rem(self.tp + step, 8)
         return {"y": other // 2, "core": lax.rem(other, 2)}
 
-    def greet(self, tp_peers):
+    def member_peer(self, step):
+        other = lax.rem(self.member + step, 16)
+        return {"y": other // 4, "core": lax.rem(other // 2, 2), "zl": lax.rem(other, 2)}
+
+    def owner(self, j):
+        ctx = 2 * j + self.core
+        return {"zh": ctx // 4, "x": lax.rem(ctx, 4), "y": self.ctx // 2, "core": lax.rem(self.ctx, 2)}
+
+    def giver(self, y):
+        return {"zh": self.tp // 4, "x": lax.rem(self.tp, 4), "y": y, "core": lax.rem(self.ctx, 2)}
+
+    def greet(self, peers):
         barrier = pltpu.get_barrier_semaphore()
-        peers = [self.beside(axis, step) for axis in ("x", "z") for step in (1, -1)]
-        if tp_peers:
-            peers += [self.tp_peer(step) for step in range(1, 8)]
+        peers = [self.beside(axis, step) for axis in ("x", "z") for step in (1, -1)] + peers
         for peer in peers:
             pl.semaphore_signal(barrier, inc=1, device_id=peer, device_id_type=MESH_ID)
-        pl.semaphore_wait(barrier, len(peers))
+        return len(peers)
 
 
 class Link:
     def __init__(self, send_sem, recv_sem):
         self.send_sem, self.recv_sem, self.open = send_sem, recv_sem, []
 
-    def copy(self, number, src, dst, device):
+    def copy(self, number, src, dst, device, landing=None):
         return pltpu.make_async_remote_copy(
             src_ref=src,
             dst_ref=dst,
             send_sem=self.send_sem.at[number],
-            recv_sem=self.recv_sem.at[number],
+            recv_sem=self.recv_sem.at[number if landing is None else landing],
             device_id=device,
             device_id_type=MESH_ID,
         )
 
-    def send(self, number, src, dst, device):
-        copy = self.copy(number, src, dst, device)
+    def send(self, number, src, dst, device, landing=None):
+        copy = self.copy(number, src, dst, device, landing)
         copy.start()
         self.open.append(copy)
 
@@ -80,7 +92,7 @@
 GATHER_COPIES = 40
 
 
-def plane_gather(place, link, piece, first=0):
+def plane_gather(place, link, piece, first=0, ready=None):
     here = (place.x, place.z)
 
     def block(part, along_f, along_s, half=None):
@@ -104,11 +116,16 @@
             link.send(number(part, "near2", g, direction), ref, ref, place.beside(s_axis(part), step))
 
     for part in (0, 1):
+        if ready is not None:
+            ready(part)
         ref = block(part, 0, 0)
         for direction, step in ((0, 1), (1, -1)):
             link.send(number(part, "near", 0, direction), ref, ref, place.beside(f_axis(part), step))
-    for part in (0, 1):
-        pass_on(part, 0)
+        if ready is not None:
+            pass_on(part, 0)
+    if ready is None:
+        for part in (0, 1):
+            pass_on(part, 0)
     for part in (0, 1):
         for direction, step in ((0, 1), (1, -1)):
             back = place.beside(f_axis(part), -step)
@@ -141,6 +158,173 @@
             for direction, step in ((0, 1), (1, -1)):
                 back = place.beside(s_axis(part), -step)
                 link.arrived(number(part, "far2", g, direction), block(part, g, 2, direction), back)
+
+
+def attention_kernel(
+    queries,
+    keys,
+    values,
+    w_out,
+    resid,
+    hres,
+    squares,
+    all_keys,
+    all_values,
+    attn,
+    given,
+    got_core,
+    kept,
+    got,
+    stats,
+    send_sem,
+    recv_sem,
+):
+    place = Place()
+    link = Link(send_sem, recv_sem)
+    barrier = pltpu.get_barrier_semaphore()
+    diagonal = place.ctx == place.tp
+    own = [jnp.logical_and(diagonal, place.y == j) for j in range(4)]
+    for j in range(4):
+
+        @pl.when(jnp.logical_not(own[j]))
+        def _():
+            for peer in (place.owner(j), place.giver(j)):
+                pl.semaphore_signal(barrier, inc=1, device_id=peer, device_id_type=MESH_ID)
+
+    members = [place.member_peer(step) for step in range(1, 16)]
+    greeted = place.greet(members)
+
+    @pl.when(diagonal)
+    def _():
+        pl.semaphore_wait(barrier, greeted + 6)
+
+    @pl.when(jnp.logical_not(diagonal))
+    def _():
+        pl.semaphore_wait(barrier, greeted + 8)
+
+    def at(x, z):
+        return ((z // 2) * 4 + x) * 2 + lax.rem(z, 2)
+
+    here = place.ctx * 2 + place.zl
+    mine = pl.ds(pl.multiple_of(place.zl * 128, 128), 128)
+    all_keys[here] = keys[mine, :]
+    all_values[here] = values[mine, :]
+
+    def key_block(x, z, part, half):
+        ref = (all_keys, all_values)[part]
+        if half is None:
+            return ref.at[at(x, z)]
+        return ref.at[at(x, z), pl.ds(half * 64, 64)]
+
+    plane_gather(place, link, key_block)
+
+    def attend(part):
+        @pl.loop(part * 3, part * 3 + 3)
+        def _(head):
+            columns = pl.ds(pl.multiple_of(head * HD, HD), HD)
+            scores = lax.dot_general(
+                queries[mine, columns],
+                all_keys[...].reshape(2048, HD),
+                (((1,), (1,)), ((), ())),
+                preferred_element_type=F32,
+            ) * HD ** (-0.5)
+            query_pos = here * 128 + lax.broadcasted_iota(jnp.int32, (128, 2048), 0)
+            key_pos = lax.broadcasted_iota(jnp.int32, (128, 2048), 1)
+            scores = jnp.where(key_pos <= query_pos, scores, -1e30)
+            probs = jnp.exp(scores - jnp.max(scores, axis=1, keepdims=True))
+            denom = jnp.sum(probs, axis=1, keepdims=True)
+            update = jnp.dot(
+                probs.astype(BF16), all_values[...].reshape(2048, HD), preferred_element_type=F32
+            )
+            attn[here, :, columns] = (update / denom).astype(BF16)
+
+    def attn_block(x, z, part, half):
+        columns = pl.ds(part * 384, 384)
+        if half is None:
+            return attn.at[at(x, z), :, columns]
+        return attn.at[at(x, z), pl.ds(half * 64, 64), columns]
+
+    plane_gather(place, link, attn_block, first=40, ready=attend)
+
+    def project(ctx):
+        rows = attn[pl.ds(ctx * 2, 2)].reshape(256, 768)
+        return jnp.dot(rows, w_out[...], preferred_element_type=F32)
+
+    partner = {"core": 1 - place.core}
+    for j in range(4):
+        given[j] = project(2 * j + 1 - place.core).astype(BF16)
+        link.send(80 + j, given.at[j], got_core.at[j], partner)
+    for j in range(4):
+        total = project(2 * j + place.core)
+        link.arrived(80 + j, got_core.at[j], partner)
+        kept[j] = (total + got_core[j].astype(F32)).astype(BF16)
+        copy = link.copy(84 + j, kept.at[j], got.at[place.y], place.owner(j), 88 + place.y)
+
+        @pl.when(own[j])
+        def _():
+            got[j] = kept[j]
+
+        @pl.when(jnp.logical_not(own[j]))
+        def _():
+            copy.start()
+
+    total = resid[...].astype(F32)
+    for j in range(4):
+
+        @pl.when(jnp.logical_not(own[j]))
+        def _():
+            link.arrived(88 + j, got.at[j], place.giver(j))
+
+        total = total + got[j].astype(F32)
+    value = total.astype(BF16)
+    hres[...] = value
+    value = value.astype(F32)
+    sums = lax.dot_general(
+        jnp.ones((8, 384), F32),
+        value * value,
+        (((1,), (1,)), ((), ())),
+        precision=lax.Precision.HIGHEST,
+        preferred_element_type=F32,
+    )
+    stats[place.member] = sums
+    for step in range(1, 16):
+        link.send(92 + step, stats.at[place.member], stats.at[place.member], members[step - 1])
+    for step in range(1, 16):
+        source = lax.rem(place.member + 16 - step, 16)
+        link.arrived(92 + step, stats.at[source], members[15 - step])
+    squares[...] = jnp.sum(stats[...], axis=0)
+    link.finish()
+    for j in range(4):
+
+        @pl.when(jnp.logical_not(own[j]))
+        def _():
+            link.copy(84 + j, kept.at[j], got.at[place.y], place.owner(j), 88 + place.y).wait_send()
+
+
+def attention(queries, keys, values, w_out, resid):
+    vmem = pl.BlockSpec(memory_space=pltpu.VMEM)
+    return pl.pallas_call(
+        attention_kernel,
+        out_shape=(jax.ShapeDtypeStruct((256, 384), BF16), jax.ShapeDtypeStruct((8, 256), F32)),
+        in_specs=[vmem] * 5,
+        out_specs=(vmem, vmem),
+        scratch_shapes=[
+            pltpu.VMEM((16, 128, HD), BF16),
+            pltpu.VMEM((16, 128, HD), BF16),
+            pltpu.VMEM((16, 128, 768), BF16),
+            pltpu.VMEM((4, 256, 384), BF16),
+            pltpu.VMEM((4, 256, 384), BF16),
+            pltpu.VMEM((4, 256, 384), BF16),
+            pltpu.VMEM((4, 256, 384), BF16),
+            pltpu.VMEM((16, 8, 256), F32),
+            pltpu.SemaphoreType.DMA((108,)),
+            pltpu.SemaphoreType.DMA((108,)),
+        ],
+        compiler_params=pltpu.CompilerParams(
+            collective_id=0, has_side_effects=True, vmem_limit_bytes=48 * 1024 * 1024
+        ),
+        name="attention",
+    )(queries, keys, values, w_out, resid)
 
 
 def experts_kernel(
@@ -173,7 +357,8 @@
     ]
     for load in loads:
         load.start()
-    place.greet(True)
+    greeted = place.greet([place.tp_peer(step) for step in range(1, 8)])
+    pl.semaphore_wait(pltpu.get_barrier_semaphore(), greeted)
 
     base = 80
     for step in range(1, 8):
@@ -359,71 +544,16 @@
     )(slots, w_gate, w_up, w_down)
 
 
-def split_up(x, dim, size):
-    dims = x.shape
-    tiles = x.reshape(*dims[:dim], size, dims[dim] // size, *dims[dim + 1 :])
-    return jnp.moveaxis(tiles, dim, 0)
-
-
-def sent_and_summed(x, axis, dim):
-    tiles = split_up(x, dim, lax.axis_size(axis))
-    arrived = lax.all_to_all(tiles, axis, split_axis=0, concat_axis=0, tiled=True)
-    return arrived.astype(jnp.float32).sum(axis=0)
-
-
-def from_everyone(x, axis):
-    size = lax.axis_size(axis)
-    return lax.all_to_all(jnp.broadcast_to(x[None], (size, *x.shape)), axis, 0, 0, tiled=True)
-
-
-def taken_together(x, axis):
-    everything = from_everyone(x, axis)
-    return jnp.sum(everything, axis=0)
-
-
 def on_device(
     resid, queries, keys, values, w_out, norm_gain, w_gate, w_up, w_down, expert_ids, route_units
 ):
     tp_size = lax.axis_size(TP)
     tok_rows = queries.shape[0]
-    heads_dev = queries.shape[1] // HD
-    kv_dev = keys.shape[1] // HD
-    group = heads_dev // kv_dev
     feat_dev = resid.shape[1]
     capacity = 3 * tok_rows // tp_size
-    first_pos = lax.axis_index(CTX) * tok_rows
-    query_heads = queries.reshape(tok_rows, kv_dev, group, HD)
-    query_pos = first_pos + jnp.arange(tok_rows, dtype=jnp.int32)
-    running_max = jnp.full((kv_dev, group, tok_rows), -1e30, jnp.float32)
-    key_piece = lax.all_gather(keys, CTX, axis=0, tiled=True)
-    value_piece = lax.all_gather(values, CTX, axis=0, tiled=True)
-    count = key_piece.shape[0]
-    key_rows = key_piece.reshape(count, kv_dev, HD)
-    value_rows = value_piece.reshape(count, kv_dev, HD)
-    scores = jnp.einsum(
-        "tkgd,nkd->kgtn", query_heads, key_rows, preferred_element_type=jnp.float32
-    ) * HD ** (-0.5)
-    key_pos = jnp.arange(count, dtype=jnp.int32)
-    allowed = (key_pos[None, :] <= query_pos[:, None])[None, None]
-    block_max = jnp.max(jnp.where(allowed, scores, -1e30), axis=-1)
-    new_max = jnp.maximum(running_max, block_max)
-    probs = jnp.where(allowed, jnp.exp(scores - new_max[..., None]), 0.0)
-    new_sum = jnp.sum(probs, axis=-1)
-    probs_b = probs.astype(jnp.bfloat16)
-    update = jnp.einsum("kgtn,nkd->kgtd", probs_b, value_rows, preferred_element_type=jnp.float32)
-    attn = (
-        (update / new_sum[..., None])
-        .transpose(2, 0, 1, 3)
-        .reshape(tok_rows, heads_dev * HD)
-        .astype(jnp.bfloat16)
-    )
-    partial_proj = jnp.dot(
-        attn, lax.all_gather(w_out, CTX, axis=1, tiled=True), preferred_element_type=jnp.float32
-    )
-    proj = sent_and_summed(partial_proj.astype(jnp.bfloat16), TP, 1)
-    hres = (resid.astype(jnp.float32) + proj).astype(jnp.bfloat16)
+    hres, squares = attention(queries, keys, values, w_out, resid)
     hfloat = hres.astype(jnp.float32)
-    square_total = taken_together(jnp.sum(hfloat * hfloat, axis=1, keepdims=True), TP_EP)
+    square_total = squares[0][:, None]
     normed = (hfloat * lax.rsqrt(square_total / D + 1e-05) * norm_gain.astype(jnp.float32)).astype(
         jnp.bfloat16
     )

time: 297 us -> 234 us (0.79)
  Pallas kernels: 143 us -> 222 us
  blocking collectives: 62.5 us -> 0 us
  waiting for transfers between devices: 45.3 us -> 0 us
  between operations: 13.6 us -> 0.06 us
  starting transfers between devices: 9.95 us -> 0 us
  matrix products: 13.2 us -> 3.56 us
    pallas_call x0 -> x1, Pallas kernels: none -> 77.6 us  [attention(): pl.pallas_call(attention_kernel, out_shape=(jax.ShapeDtypeStruct((256, 38...]
    all_gather x2 -> x0, blocking collectives: 62.5 us -> none  [the longest x1 31.8 us: on_device(): key_piece = lax.all_gather(keys, CTX, axis=0, tiled=True)]
    all_to_all x2 -> x0, waiting for transfers between devices: 25.4 us -> none  [the longest x1 19.6 us: sent_and_summed(): lax.all_to_all(tiles, axis, split_axis=0, concat_axis=0, tiled=True)]
    all_gather x1 -> x0, waiting for transfers between devices: 19.2 us -> none  [on_device(): lax.all_gather(w_out, CTX, axis=1, tiled=True)]
    all_to_all x2 -> x0, starting transfers between devices: 9.94 us -> none  [the longest x1 5.68 us: sent_and_summed(): lax.all_to_all(tiles, axis, split_axis=0, concat_axis=0, tiled=True)]
    dot_general x3 -> x0, matrix products: 8.68 us -> none  [the longest x1 3.75 us: on_device(): jnp.dot(attn, lax.all_gather(w_out, CTX, axis=1, tiled=True), preferred_e...]
    reduce_sum x4 -> x0, other arithmetic: 3.57 us -> none  [the longest x1 2.58 us: on_device(): new_sum = jnp.sum(probs, axis=-1)]
  transfers between devices with their start and end apart: 3 -> 0, of which waited for: 3 -> 0; matrix products, arithmetic and copies ran while one was open for 4% -> 0% of each run, Pallas kernels for 0% -> 0%
where the time goes in v2:
time: 234 us
  Pallas kernels  222 us (95%)
  local copies, waits for them, and re-layouts  4.92 us (2%)
  matrix products  3.56 us (2%)
  other arithmetic  3.53 us (2%)
    pallas_call x1, Pallas kernels, experts(): pl.pallas_call(experts_kernel, out_shape=jax.ShapeDtypeStruct((8, 96, 384...  144 us
    pallas_call x1, Pallas kernels, attention(): pl.pallas_call(attention_kernel, out_shape=(jax.ShapeDtypeStruct((256, 38...  77.6 us

profile of v2, /device:TPU:1, one launch (start us, length us, event | category | flops | bytes accessed | tf_op | source)
XLA Modules:
  0.0 233.6 jit_solution(559170279633741683)
XLA Ops:
  0.0 0.7 convert_reduce_fusion
  0.7 0.6 reduce-window.6
  1.3 0.2 slice_reduce_fusion
  1.5 0.1 bitcast_subtract_fusion
  1.6 0.7 select_reduce_fusion
  2.3 0.7 multiply_add_fusion
  3.0 0.0 copy-start
  3.0 1.1 copy-done
  4.1 0.0 copy-start.1
  4.1 1.0 copy-done.1
  5.1 0.0 copy-start.2
  5.1 0.9 copy-done.2
  6.0 0.0 copy-start.3
  6.0 0.8 copy-done.3
  6.8 0.0 copy-start.4
  6.8 0.8 copy-done.4
  7.7 77.6 %attention.1 = (bf16[256,384]{1,0:T(8,128)(2,1)S(1)}, f32[8,256]{1,0:T(8,128)S(1)}) custom-call(bf16[256,768]{1,0:T(8,128)(2,1)S(1)} %copy-done.1, bf16[256,128]{1,0:T(8,128)(2,1)S(1)} %copy-done.3, bf16[256,128]{1,0:T(8,128)(2,1)S(1)} %copy-done.4, bf16[768,384]{1,0:T(8,128)(2,1)S(1)} %copy-done, bf16[256,384]{1,0:T(8,128)(2,1)S(1)} %copy-done.2), custom_call_target="tpu_custom_call" | custom-call | tf_op jit(solution)/shard_map/attention/pallas_call | solution.py:306
  85.3 0.0 copy-start.5
  85.3 0.7 convert_element_type.32
  86.1 0.0 copy-done.5
  86.1 1.3 convolution_convert_fusion
  87.3 0.0 copy-start.6
  87.3 143.9 %experts.1 = bf16[8,96,384]{2,1,0:T(8,128)(2,1)} custom-call(bf16[8,96,384]{2,1,0:T(8,128)(2,1)} %bitcast.20, bf16[6144,512]{1,0:T(8,128)(2,1)} %bitcast.16, bf16[6144,512]{1,0:T(8,128)(2,1)} %bitcast.17, bf16[512,6144]{1,0:T(8,128)(2,1)} %bitcast.18), custom_call_target="tpu_custom_call" | custom-call | tf_op jit(solution)/shard_map/experts/pallas_call | solution.py:518
  231.3 0.0 copy-done.6
  231.3 2.3 fusion
  (7 shorter events, 0.1 us)
Async XLA Ops:
  3.0 1.1 copy-start
  4.1 1.0 copy-start.1
  5.1 0.9 copy-start.2
  6.0 0.8 copy-start.3
  6.8 0.8 copy-start.4
  85.3 0.8 copy-start.5
  87.3 144.0 %copy-start.6 = (s32[256,2]{0,1:T(2,128)S(1)}, s32[256,2]{0,1:T(2,128)}, u32[]{:S(2)}) copy-start(s32[256,2]{0,1:T(2,128)} %param.21) | copy-start | bytes 6148

commit v3 on v2

--- a/solution.py
+++ b/solution.py
@@ -46,12 +46,8 @@
         other = lax.rem(self.member + step, 16)
         return {"y": other // 4, "core": lax.rem(other // 2, 2), "zl": lax.rem(other, 2)}
 
-    def owner(self, j):
-        ctx = 2 * j + self.core
-        return {"zh": ctx // 4, "x": lax.rem(ctx, 4), "y": self.ctx // 2, "core": lax.rem(self.ctx, 2)}
-
-    def giver(self, y):
-        return {"zh": self.tp // 4, "x": lax.rem(self.tp, 4), "y": y, "core": lax.rem(self.ctx, 2)}
+    def mirror(self):
+        return {"zh": self.tp // 4, "x": lax.rem(self.tp, 4), "y": self.ctx // 2, "core": lax.rem(self.ctx, 2)}
 
     def greet(self, peers):
         barrier = pltpu.get_barrier_semaphore()
@@ -92,7 +88,7 @@
 GATHER_COPIES = 40
 
 
-def plane_gather(place, link, piece, first=0, ready=None):
+def plane_gather(place, link, piece, first=0, ready=None, seen=None):
     here = (place.x, place.z)
 
     def block(part, along_f, along_s, half=None):
@@ -143,6 +139,16 @@
             ref = block(part, g, -step, direction)
             link.send(number(part, "far2", g, direction), ref, ref, place.beside(s_axis(part), step))
 
+    def last(g):
+        for part in (0, 1):
+            for direction, step in ((0, 1), (1, -1)):
+                back = place.beside(s_axis(part), -step)
+                link.arrived(number(part, "far2", g, direction), block(part, g, 2, direction), back)
+
+    def use(part, along_z):
+        if seen is not None:
+            seen(part, along_z)
+
     for part in (0, 1):
         relay(part, 0)
     for part in (0, 1):
@@ -150,14 +156,23 @@
             back = place.beside(f_axis(part), -step)
             link.arrived(number(part, "far", 0, direction), block(part, 2, 0, direction), back)
         pass_on(part, 2)
-    for g in (-1, 1, 2):
+    use(0, 0)
+    for g in (-1, 1):
         for part in (0, 1):
             relay(part, g)
-    for g in (0, -1, 1, 2):
-        for part in (0, 1):
-            for direction, step in ((0, 1), (1, -1)):
-                back = place.beside(s_axis(part), -step)
-                link.arrived(number(part, "far2", g, direction), block(part, g, 2, direction), back)
+    last(0)
+    use(1, 0)
+    for part in (0, 1):
+        relay(part, 2)
+    use(0, -1)
+    use(0, 1)
+    for g in (-1, 1):
+        last(g)
+    use(1, -1)
+    use(1, 1)
+    last(2)
+    use(0, 2)
+    use(1, 2)
 
 
 def attention_kernel(
@@ -183,24 +198,17 @@
     link = Link(send_sem, recv_sem)
     barrier = pltpu.get_barrier_semaphore()
     diagonal = place.ctx == place.tp
-    own = [jnp.logical_and(diagonal, place.y == j) for j in range(4)]
-    for j in range(4):
-
-        @pl.when(jnp.logical_not(own[j]))
-        def _():
-            for peer in (place.owner(j), place.giver(j)):
-                pl.semaphore_signal(barrier, inc=1, device_id=peer, device_id_type=MESH_ID)
-
     members = [place.member_peer(step) for step in range(1, 16)]
     greeted = place.greet(members)
 
     @pl.when(diagonal)
     def _():
-        pl.semaphore_wait(barrier, greeted + 6)
+        pl.semaphore_wait(barrier, greeted)
 
     @pl.when(jnp.logical_not(diagonal))
     def _():
-        pl.semaphore_wait(barrier, greeted + 8)
+        pl.semaphore_signal(barrier, inc=1, device_id=place.mirror(), device_id_type=MESH_ID)
+        pl.semaphore_wait(barrier, greeted + 1)
 
     def at(x, z):
         return ((z // 2) * 4 + x) * 2 + lax.rem(z, 2)
@@ -251,31 +259,33 @@
         return jnp.dot(rows, w_out[...], preferred_element_type=F32)
 
     partner = {"core": 1 - place.core}
-    for j in range(4):
-        given[j] = project(2 * j + 1 - place.core).astype(BF16)
-        link.send(80 + j, given.at[j], got_core.at[j], partner)
-    for j in range(4):
+    order = [wrapped(place.y + step) for step in (2, 1, -1, 0)]
+    for i, j in enumerate(order):
+        given[i] = project(2 * j + 1 - place.core).astype(BF16)
+        link.send(80 + i, given.at[i], got_core.at[i], partner)
+    for i, j in enumerate(order):
         total = project(2 * j + place.core)
-        link.arrived(80 + j, got_core.at[j], partner)
-        kept[j] = (total + got_core[j].astype(F32)).astype(BF16)
-        copy = link.copy(84 + j, kept.at[j], got.at[place.y], place.owner(j), 88 + place.y)
-
-        @pl.when(own[j])
-        def _():
-            got[j] = kept[j]
-
-        @pl.when(jnp.logical_not(own[j]))
-        def _():
-            copy.start()
-
-    total = resid[...].astype(F32)
-    for j in range(4):
-
-        @pl.when(jnp.logical_not(own[j]))
-        def _():
-            link.arrived(88 + j, got.at[j], place.giver(j))
-
-        total = total + got[j].astype(F32)
+        link.arrived(80 + i, got_core.at[i], partner)
+        total = total + got_core[i].astype(F32)
+        if i < 3:
+            kept[i] = total.astype(BF16)
+            link.send(84 + i, kept.at[i], got.at[i], {"y": j})
+    for i, step in enumerate((2, 1, -1)):
+        link.arrived(84 + i, got.at[i], {"y": wrapped(place.y - step)})
+        total = total + got[i].astype(F32)
+    kept[3] = total.astype(BF16)
+    move = link.copy(87, kept.at[3], got.at[3], place.mirror())
+
+    @pl.when(diagonal)
+    def _():
+        got[3] = kept[3]
+
+    @pl.when(jnp.logical_not(diagonal))
+    def _():
+        move.start()
+        link.arrived(87, got.at[3], place.mirror())
+
+    total = resid[...].astype(F32) + got[3].astype(F32)
     value = total.astype(BF16)
     hres[...] = value
     value = value.astype(F32)
@@ -294,11 +304,10 @@
         link.arrived(92 + step, stats.at[source], members[15 - step])
     squares[...] = jnp.sum(stats[...], axis=0)
     link.finish()
-    for j in range(4):
-
-        @pl.when(jnp.logical_not(own[j]))
-        def _():
-            link.copy(84 + j, kept.at[j], got.at[place.y], place.owner(j), 88 + place.y).wait_send()
+
+    @pl.when(jnp.logical_not(diagonal))
+    def _():
+        move.wait_send()
 
 
 def attention(queries, keys, values, w_out, resid):
@@ -355,8 +364,8 @@
         pltpu.make_async_copy(src, dst, load_sem.at[i])
         for i, (src, dst) in enumerate(((w_gate, gate_w), (w_up, up_w), (w_down, down_w)))
     ]
-    for load in loads:
-        load.start()
+    loads[0].start()
+    loads[1].start()
     greeted = place.greet([place.tp_peer(step) for step in range(1, 8)])
     pl.semaphore_wait(pltpu.get_barrier_semaphore(), greeted)
 
@@ -374,25 +383,29 @@
             return rows.at[x, z, pl.ds(part * 4, 4)]
         return rows.at[x, z, pl.ds(part * 4 + half * 2, 2)]
 
-    plane_gather(place, link, block_of_rows)
-
-    loads[0].wait()
-    loads[1].wait()
+    gate_acc[...] = jnp.zeros_like(gate_acc)
+    up_acc[...] = jnp.zeros_like(up_acc)
+
+    def use_rows(part, along_z):
+        if (part, along_z) == (0, 0):
+            loads[0].wait()
+            loads[1].wait()
+            loads[2].start()
+        z = wrapped(place.z + along_z)
+        zh, e = z // 2, lax.rem(z, 2)
+
+        @pl.loop(part * 2, part * 2 + 2)
+        def _(pair):
+            left = jnp.concatenate([rows[:, z, 2 * pair + i].reshape(384, 384) for i in range(2)], axis=1)
+            spans = [pl.ds(pl.multiple_of((4 * pair + 2 * i + e) * 384, 384), 384) for i in range(2)]
+            for acc, weights in ((gate_acc, gate_w), (up_acc, up_w)):
+                right = jnp.concatenate([weights[span, :] for span in spans], axis=0)
+                acc[zh] += jnp.dot(left, right, preferred_element_type=F32)
+
+    plane_gather(place, link, block_of_rows, seen=use_rows)
     for zh in range(2):
-        gate_acc[...] = jnp.zeros_like(gate_acc)
-        up_acc[...] = jnp.zeros_like(up_acc)
-
-        @pl.loop(0, 8)
-        def _(t):
-            even = rows[:, 2 * zh, t].reshape(384, 384)
-            odd = rows[:, 2 * zh + 1, t].reshape(384, 384)
-            left = jnp.concatenate([even, odd], axis=1)
-            span = pl.ds(pl.multiple_of(t * 768, 768), 768)
-            gate_acc[...] += jnp.dot(left, gate_w[span, :], preferred_element_type=F32)
-            up_acc[...] += jnp.dot(left, up_w[span, :], preferred_element_type=F32)
-
-        gate = gate_acc[...]
-        value = gate / (1.0 + jnp.exp(-gate)) * up_acc[...]
+        gate = gate_acc[zh]
+        value = gate / (1.0 + jnp.exp(-gate)) * up_acc[zh]
         hidden[pl.ds(zh * 4, 4)] = value.astype(BF16).reshape(4, 96, 512)
     loads[2].wait()
 
@@ -484,12 +497,14 @@
         for part in (0, 1):
             compute(part, g)
             outer[part][g].far()
-    for g in FAR_FIRST:
+    for g in (2, 1, -1):
         for part in (0, 1):
             outer[part][g].near()
     for part in (0, 1):
         outer[part][2].end()
         inner[part].far()
+    for part in (0, 1):
+        outer[part][0].near()
     for part in (0, 1):
         outer[part][1].end()
         outer[part][-1].end()
@@ -525,8 +540,8 @@
             pltpu.VMEM((6144, 512), BF16),
             pltpu.VMEM((6144, 512), BF16),
             pltpu.VMEM((512, 6144), BF16),
-            pltpu.VMEM((384, 512), F32),
-            pltpu.VMEM((384, 512), F32),
+            pltpu.VMEM((2, 384, 512), F32),
+            pltpu.VMEM((2, 384, 512), F32),
             pltpu.VMEM((8, 96, 512), BF16),
             pltpu.VMEM((4, 4, 8, 96, 384), BF16),
             pltpu.VMEM((2, 5, 2, 2, 96, 384), BF16),

time: 234 us -> 217 us (0.927)
  Pallas kernels: 222 us -> 204 us
    pallas_call x1, Pallas kernels: 144 us -> 131 us  [experts(): pl.pallas_call(experts_kernel, out_shape=jax.ShapeDtypeStruct((8, 96, 384...]
    pallas_call x1, Pallas kernels: 77.6 us -> 72.9 us  [attention(): pl.pallas_call(attention_kernel, out_shape=(jax.ShapeDtypeStruct((256, 38...]
where the time goes in v3:
time: 217 us; the launch traced here: 216 us
  Pallas kernels  204 us (94%)
  local copies, waits for them, and re-layouts  4.92 us (2%)
  matrix products  3.56 us (2%)
  other arithmetic  3.53 us (2%)
    pallas_call x1, Pallas kernels, experts(): pl.pallas_call(experts_kernel, out_shape=jax.ShapeDtypeStruct((8, 96, 384...  131 us
    pallas_call x1, Pallas kernels, attention(): pl.pallas_call(attention_kernel, out_shape=(jax.ShapeDtypeStruct((256, 38...  72.9 us
    unnamed x14, local copies, waits for them, and re-layouts  4.67 us

profile of v3, /device:TPU:1, one launch (start us, length us, event | category | flops | bytes accessed | tf_op | source)
XLA Modules:
  0.0 216.2 jit_solution(6170820084393488596)
XLA Ops:
  0.0 0.7 convert_reduce_fusion
  0.7 0.6 reduce-window.6
  1.3 0.2 slice_reduce_fusion
  1.5 0.1 bitcast_subtract_fusion
  1.6 0.7 select_reduce_fusion
  2.3 0.7 multiply_add_fusion
  3.0 0.0 copy-start
  3.0 1.1 copy-done
  4.1 0.0 copy-start.1
  4.1 1.0 copy-done.1
  5.1 0.0 copy-start.2
  5.1 0.9 copy-done.2
  6.0 0.0 copy-start.3
  6.0 0.8 copy-done.3
  6.8 0.0 copy-start.4
  6.8 0.8 copy-done.4
  7.7 72.9 %attention.1 = (bf16[256,384]{1,0:T(8,128)(2,1)S(1)}, f32[8,256]{1,0:T(8,128)S(1)}) custom-call(bf16[256,768]{1,0:T(8,128)(2,1)S(1)} %copy-done.1, bf16[256,128]{1,0:T(8,128)(2,1)S(1)} %copy-done.3, bf16[256,128]{1,0:T(8,128)(2,1)S(1)} %copy-done.4, bf16[768,384]{1,0:T(8,128)(2,1)S(1)} %copy-done, bf16[256,384]{1,0:T(8,128)(2,1)S(1)} %copy-done.2), custom_call_target="tpu_custom_call" | custom-call | tf_op jit(solution)/shard_map/attention/pallas_call | solution.py:315
  80.6 0.0 copy-start.5
  80.6 0.7 convert_element_type.32
  81.3 0.0 copy-done.5
  81.3 1.3 convolution_convert_fusion
  82.6 0.0 copy-start.6
  82.6 131.3 %experts.1 = bf16[8,96,384]{2,1,0:T(8,128)(2,1)} custom-call(bf16[8,96,384]{2,1,0:T(8,128)(2,1)} %bitcast.20, bf16[6144,512]{1,0:T(8,128)(2,1)} %bitcast.16, bf16[6144,512]{1,0:T(8,128)(2,1)} %bitcast.17, bf16[512,6144]{1,0:T(8,128)(2,1)} %bitcast.18), custom_call_target="tpu_custom_call" | custom-call | tf_op jit(solution)/shard_map/experts/pallas_call | solution.py:533
  213.9 0.0 copy-done.6
  213.9 2.3 %fusion = bf16[256,384]{1,0:T(8,128)(2,1)} fusion(bf16[768,384]{1,0:T(8,128)(2,1)} %bitcast.19, bf16[256,384]{1,0:T(8,128)(2,1)} %copy-done.5, s32[256]{0:T(256)S(1)} %bitcast.26, s32[256]{0:T(256)S(1)} %bitcast.24, bf16[256]{0:T(256)(128)(2,1)S(1)} %get-tuple-element.10, bf16[256]{0:T(256)(128)(2,1)S(1)} %get-tuple-element.9), kind=kOutput, calls=%fused_computation.2 | convolution fusion | flops 152862720 | bytes 986112 | tf_op jit(solution)/shard_map/dot_general | solution.py:591
  (7 shorter events, 0.1 us)
Async XLA Ops:
  3.0 1.1 copy-start
  4.1 1.0 copy-start.1
  5.1 0.9 copy-start.2
  6.0 0.8 copy-start.3
  6.8 0.8 copy-start.4
  80.6 0.8 copy-start.5
  82.6 131.3 %copy-start.6 = (s32[256,2]{0,1:T(2,128)S(1)}, s32[256,2]{0,1:T(2,128)}, u32[]{:S(2)}) copy-start(s32[256,2]{0,1:T(2,128)} %param.21) | copy-start | bytes 6148

commit v4 on v3

--- a/solution.py
+++ b/solution.py
@@ -88,7 +88,7 @@
 GATHER_COPIES = 40
 
 
-def plane_gather(place, link, piece, first=0, ready=None, seen=None):
+def plane_gather(place, link, piece, first=0, ready=None, seen=None, busy=None):
     here = (place.x, place.z)
 
     def block(part, along_f, along_s, half=None):
@@ -122,6 +122,8 @@
     if ready is None:
         for part in (0, 1):
             pass_on(part, 0)
+    if busy is not None:
+        busy()
     for part in (0, 1):
         for direction, step in ((0, 1), (1, -1)):
             back = place.beside(f_axis(part), -step)
@@ -175,31 +177,80 @@
     use(1, 2)
 
 
-def attention_kernel(
+def layer_kernel(
+    resid_hbm,
+    queries_hbm,
+    keys_hbm,
+    values_hbm,
+    w_out_hbm,
+    gain_hbm,
+    w_gate,
+    w_up,
+    w_down,
+    ids_hbm,
+    units_hbm,
+    out,
+    resid,
     queries,
     keys,
     values,
     w_out,
-    resid,
-    hres,
-    squares,
+    ids,
+    units,
     all_keys,
     all_values,
-    attn,
-    given,
-    got_core,
-    kept,
-    got,
-    stats,
+    gains,
+    picks,
+    combine,
+    hres,
+    slots,
+    rows,
+    gate_w,
+    up_w,
+    down_w,
+    row_squares,
+    gate_acc,
+    up_acc,
+    hidden,
+    partial,
+    got_half,
+    got_part,
+    result,
+    returned,
+    load_sem,
     send_sem,
     recv_sem,
 ):
     place = Place()
     link = Link(send_sem, recv_sem)
+    pieces = Link(send_sem, recv_sem)
+    pairs = (
+        (keys_hbm, keys),
+        (values_hbm, values),
+        (queries_hbm, queries),
+        (gain_hbm, gains.at[place.member]),
+        (ids_hbm, ids),
+        (units_hbm, units),
+        (w_out_hbm, w_out),
+        (resid_hbm, resid),
+        (w_down, down_w),
+        (w_gate, gate_w),
+        (w_up, up_w),
+    )
+    loads = [pltpu.make_async_copy(src, dst, load_sem.at[i]) for i, (src, dst) in enumerate(pairs)]
+    for load in loads[:9]:
+        load.start()
     barrier = pltpu.get_barrier_semaphore()
     diagonal = place.ctx == place.tp
     members = [place.member_peer(step) for step in range(1, 16)]
     greeted = place.greet(members)
+    for load in loads[:2]:
+        load.wait()
+
+    here = place.ctx * 2 + place.zl
+    mine = pl.ds(pl.multiple_of(place.zl * 128, 128), 128)
+    all_keys[here] = keys[mine, :]
+    all_values[here] = values[mine, :]
 
     @pl.when(diagonal)
     def _():
@@ -212,11 +263,6 @@
 
     def at(x, z):
         return ((z // 2) * 4 + x) * 2 + lax.rem(z, 2)
-
-    here = place.ctx * 2 + place.zl
-    mine = pl.ds(pl.multiple_of(place.zl * 128, 128), 128)
-    all_keys[here] = keys[mine, :]
-    all_values[here] = values[mine, :]
 
     def key_block(x, z, part, half):
         ref = (all_keys, all_values)[part]
@@ -224,12 +270,43 @@
             return ref.at[at(x, z)]
         return ref.at[at(x, z), pl.ds(half * 64, 64)]
 
-    plane_gather(place, link, key_block)
+    def route():
+        loads[3].wait()
+        for step in range(1, 16):
+            ref = gains.at[place.member]
+            link.send(88 + step, ref, ref, members[step - 1])
+        loads[4].wait()
+        loads[5].wait()
+        lanes = lax.broadcasted_iota(jnp.int32, (256, 128), 1)
+        named = [ids[:, k : k + 1] == lanes for k in range(2)]
+        tokens = jnp.where(named[0] | named[1], 1.0, 0.0).astype(BF16)
+        row = lax.broadcasted_iota(jnp.int32, (256, 256), 0)
+        column = lax.broadcasted_iota(jnp.int32, (256, 256), 1)
+        before = jnp.where(column < row, 1.0, 0.0).astype(BF16)
+        earlier = jnp.dot(before, tokens, preferred_element_type=F32)
+        amounts = units[...].astype(F32)
+        weights = (amounts / jnp.sum(amounts, axis=1, keepdims=True)).astype(BF16).astype(F32)
+        slot_ids = lax.broadcasted_iota(jnp.int32, (256, 768), 1).astype(F32)
+        hits = []
+        for k in range(2):
+            slot = jnp.sum(jnp.where(named[k], earlier, 0.0), axis=1, keepdims=True)
+            code = ids[:, k : k + 1].astype(F32) * 96.0 + slot
+            hits.append(slot_ids == code)
+        picks[...] = jnp.where(hits[0] | hits[1], 1.0, 0.0).astype(BF16)
+        combine[...] = (
+            jnp.where(hits[0], weights[:, 0:1], 0.0) + jnp.where(hits[1], weights[:, 1:2], 0.0)
+        ).astype(BF16)
+
+    plane_gather(place, link, key_block, busy=route)
+    loads[2].wait()
+
+    def attn_rows(part, block, start, count):
+        return pl.ds(pl.multiple_of(part * 2048 + block * 128 + start, 64), count), pl.ds(0, 384)
 
     def attend(part):
-        @pl.loop(part * 3, part * 3 + 3)
-        def _(head):
-            columns = pl.ds(pl.multiple_of(head * HD, HD), HD)
+        @pl.loop(0, 3)
+        def _(i):
+            columns = pl.ds(pl.multiple_of((part * 3 + i) * HD, HD), HD)
             scores = lax.dot_general(
                 queries[mine, columns],
                 all_keys[...].reshape(2048, HD),
@@ -244,136 +321,86 @@
             update = jnp.dot(
                 probs.astype(BF16), all_values[...].reshape(2048, HD), preferred_element_type=F32
             )
-            attn[here, :, columns] = (update / denom).astype(BF16)
+            where = attn_rows(part, here, 0, 128)[0]
+            gate_w[where, pl.ds(pl.multiple_of(i * HD, HD), HD)] = (update / denom).astype(BF16)
 
     def attn_block(x, z, part, half):
-        columns = pl.ds(part * 384, 384)
         if half is None:
-            return attn.at[at(x, z), :, columns]
-        return attn.at[at(x, z), pl.ds(half * 64, 64), columns]
+            return gate_w.at[attn_rows(part, at(x, z), 0, 128)]
+        return gate_w.at[attn_rows(part, at(x, z), half * 64, 64)]
 
     plane_gather(place, link, attn_block, first=40, ready=attend)
 
+    loads[6].wait()
+
     def project(ctx):
-        rows = attn[pl.ds(ctx * 2, 2)].reshape(256, 768)
-        return jnp.dot(rows, w_out[...], preferred_element_type=F32)
+        total = None
+        for part in (0, 1):
+            term = jnp.dot(
+                gate_w[pl.ds(pl.multiple_of(part * 2048 + ctx * 256, 256), 256), pl.ds(0, 384)],
+                w_out[pl.ds(part * 384, 384), :],
+                preferred_element_type=F32,
+            )
+            total = term if total is None else total + term
+        return total
+
+    def piece(k):
+        return up_w.at[pl.ds(k * 256, 256), pl.ds(0, 384)]
 
     partner = {"core": 1 - place.core}
     order = [wrapped(place.y + step) for step in (2, 1, -1, 0)]
     for i, j in enumerate(order):
-        given[i] = project(2 * j + 1 - place.core).astype(BF16)
-        link.send(80 + i, given.at[i], got_core.at[i], partner)
+        piece(i)[...] = project(2 * j + 1 - place.core).astype(BF16)
+        pieces.send(80 + i, piece(i), piece(4 + i), partner)
     for i, j in enumerate(order):
         total = project(2 * j + place.core)
-        link.arrived(80 + i, got_core.at[i], partner)
-        total = total + got_core[i].astype(F32)
+        pieces.arrived(80 + i, piece(4 + i), partner)
+        total = total + piece(4 + i)[...].astype(F32)
         if i < 3:
-            kept[i] = total.astype(BF16)
-            link.send(84 + i, kept.at[i], got.at[i], {"y": j})
+            piece(8 + i)[...] = total.astype(BF16)
+            pieces.send(84 + i, piece(8 + i), piece(12 + i), {"y": j})
+    link.finish()
+    loads[9].start()
     for i, step in enumerate((2, 1, -1)):
-        link.arrived(84 + i, got.at[i], {"y": wrapped(place.y - step)})
-        total = total + got[i].astype(F32)
-    kept[3] = total.astype(BF16)
-    move = link.copy(87, kept.at[3], got.at[3], place.mirror())
+        pieces.arrived(84 + i, piece(12 + i), {"y": wrapped(place.y - step)})
+        total = total + piece(12 + i)[...].astype(F32)
+    piece(11)[...] = total.astype(BF16)
+    move = pieces.copy(87, piece(11), piece(15), place.mirror())
 
     @pl.when(diagonal)
     def _():
-        got[3] = kept[3]
+        piece(15)[...] = piece(11)[...]
 
     @pl.when(jnp.logical_not(diagonal))
     def _():
         move.start()
-        link.arrived(87, got.at[3], place.mirror())
-
-    total = resid[...].astype(F32) + got[3].astype(F32)
-    value = total.astype(BF16)
-    hres[...] = value
-    value = value.astype(F32)
-    sums = lax.dot_general(
-        jnp.ones((8, 384), F32),
-        value * value,
-        (((1,), (1,)), ((), ())),
-        precision=lax.Precision.HIGHEST,
-        preferred_element_type=F32,
-    )
-    stats[place.member] = sums
-    for step in range(1, 16):
-        link.send(92 + step, stats.at[place.member], stats.at[place.member], members[step - 1])
-    for step in range(1, 16):
-        source = lax.rem(place.member + 16 - step, 16)
-        link.arrived(92 + step, stats.at[source], members[15 - step])
-    squares[...] = jnp.sum(stats[...], axis=0)
-    link.finish()
-
-    @pl.when(jnp.logical_not(diagonal))
-    def _():
-        move.wait_send()
-
-
-def attention(queries, keys, values, w_out, resid):
-    vmem = pl.BlockSpec(memory_space=pltpu.VMEM)
-    return pl.pallas_call(
-        attention_kernel,
-        out_shape=(jax.ShapeDtypeStruct((256, 384), BF16), jax.ShapeDtypeStruct((8, 256), F32)),
-        in_specs=[vmem] * 5,
-        out_specs=(vmem, vmem),
-        scratch_shapes=[
-            pltpu.VMEM((16, 128, HD), BF16),
-            pltpu.VMEM((16, 128, HD), BF16),
-            pltpu.VMEM((16, 128, 768), BF16),
-            pltpu.VMEM((4, 256, 384), BF16),
-            pltpu.VMEM((4, 256, 384), BF16),
-            pltpu.VMEM((4, 256, 384), BF16),
-            pltpu.VMEM((4, 256, 384), BF16),
-            pltpu.VMEM((16, 8, 256), F32),
-            pltpu.SemaphoreType.DMA((108,)),
-            pltpu.SemaphoreType.DMA((108,)),
-        ],
-        compiler_params=pltpu.CompilerParams(
-            collective_id=0, has_side_effects=True, vmem_limit_bytes=48 * 1024 * 1024
-        ),
-        name="attention",
-    )(queries, keys, values, w_out, resid)
-
-
-def experts_kernel(
-    slots,
-    w_gate,
-    w_up,
-    w_down,
-    out,
-    rows,
-    gate_w,
-    up_w,
-    down_w,
-    gate_acc,
-    up_acc,
-    hidden,
-    partial,
-    got_half,
-    got_part,
-    result,
-    returned,
-    load_sem,
-    send_sem,
-    recv_sem,
-):
-    place = Place()
-    link = Link(send_sem, recv_sem)
-    loads = [
-        pltpu.make_async_copy(src, dst, load_sem.at[i])
-        for i, (src, dst) in enumerate(((w_gate, gate_w), (w_up, up_w), (w_down, down_w)))
-    ]
-    loads[0].start()
-    loads[1].start()
-    greeted = place.greet([place.tp_peer(step) for step in range(1, 8)])
-    pl.semaphore_wait(pltpu.get_barrier_semaphore(), greeted)
-
-    base = 80
+        pieces.arrived(87, piece(15), place.mirror())
+
+    loads[7].wait()
+    hres[...] = (resid[...].astype(F32) + piece(15)[...].astype(F32)).astype(BF16)
+    dispatched = lax.dot_general(
+        picks[...], hres[...], (((0,), (0,)), ((), ())), preferred_element_type=F32
+    ).astype(BF16)
+    slots[...] = dispatched.reshape(8, 96, 384)
+
+    base = 104
     for step in range(1, 8):
         target = lax.rem(place.tp + step, 8)
         link.send(base + step, slots.at[target], rows.at[place.x, place.z, place.tp], place.tp_peer(step))
     rows[place.x, place.z, place.tp] = slots[place.tp]
+
+    @pl.when(jnp.logical_not(diagonal))
+    def _():
+        move.wait_send()
+
+    pieces.finish()
+    loads[10].start()
+    gate_acc[...] = jnp.zeros_like(gate_acc)
+    up_acc[...] = jnp.zeros_like(up_acc)
+    row_squares[...] = jnp.zeros_like(row_squares)
+    for step in range(1, 16):
+        source = lax.rem(place.member + 16 - step, 16)
+        link.arrived(88 + step, gains.at[source], members[15 - step])
     for step in range(1, 8):
         source = lax.rem(place.tp + 8 - step, 8)
         link.arrived(base + step, rows.at[place.x, place.z, source], place.tp_peer(8 - step))
@@ -383,31 +410,38 @@
             return rows.at[x, z, pl.ds(part * 4, 4)]
         return rows.at[x, z, pl.ds(part * 4 + half * 2, 2)]
 
-    gate_acc[...] = jnp.zeros_like(gate_acc)
-    up_acc[...] = jnp.zeros_like(up_acc)
-
     def use_rows(part, along_z):
         if (part, along_z) == (0, 0):
-            loads[0].wait()
-            loads[1].wait()
-            loads[2].start()
+            loads[9].wait()
+            loads[10].wait()
         z = wrapped(place.z + along_z)
         zh, e = z // 2, lax.rem(z, 2)
 
         @pl.loop(part * 2, part * 2 + 2)
         def _(pair):
-            left = jnp.concatenate([rows[:, z, 2 * pair + i].reshape(384, 384) for i in range(2)], axis=1)
+            lefts = []
+            squares = row_squares[zh]
+            for i in range(2):
+                t = 2 * pair + i
+                value = rows[:, z, t].reshape(384, 384).astype(F32)
+                lefts.append((value * gains[2 * t + e, 0:1, :]).astype(BF16))
+                square = value * value
+                squares = squares + square[:, 0:128] + square[:, 128:256] + square[:, 256:384]
+            row_squares[zh] = squares
+            left = jnp.concatenate(lefts, axis=1)
             spans = [pl.ds(pl.multiple_of((4 * pair + 2 * i + e) * 384, 384), 384) for i in range(2)]
             for acc, weights in ((gate_acc, gate_w), (up_acc, up_w)):
                 right = jnp.concatenate([weights[span, :] for span in spans], axis=0)
                 acc[zh] += jnp.dot(left, right, preferred_element_type=F32)
 
-    plane_gather(place, link, block_of_rows, seen=use_rows)
+    plane_gather(place, link, block_of_rows, first=112, seen=use_rows)
     for zh in range(2):
-        gate = gate_acc[zh]
-        value = gate / (1.0 + jnp.exp(-gate)) * up_acc[zh]
+        mean = jnp.sum(row_squares[zh], axis=1, keepdims=True) / D
+        scale = lax.rsqrt(mean + 1e-05)
+        gate = gate_acc[zh] * scale
+        value = gate / (1.0 + jnp.exp(-gate)) * (up_acc[zh] * scale)
         hidden[pl.ds(zh * 4, 4)] = value.astype(BF16).reshape(4, 96, 512)
-    loads[2].wait()
+    loads[8].wait()
 
     def compute(part, g):
         if part == 0:
@@ -451,7 +485,7 @@
     class Ring:
         def __init__(self, part, stage, axis, at):
             self.part, self.stage, self.axis, self.at = part, stage, axis, at
-            self.number = 100 + (part * 5 + stage) * 4
+            self.number = 152 + (part * 5 + stage) * 4
 
         def far(self):
             for direction, step in ((0, 1), (1, -1)):
@@ -509,7 +543,7 @@
         outer[part][1].end()
         outer[part][-1].end()
         inner[part].near()
-    base = 88
+    base = 192
     for part in (0, 1):
         outer[part][0].end()
         gots = inner[part].receive()
@@ -525,21 +559,40 @@
         source = lax.rem(place.tp + 8 - step, 8)
         link.arrived(base + step, returned.at[source], place.tp_peer(8 - step))
     link.finish()
-    out[...] = returned[...]
-
-
-def experts(slots, w_gate, w_up, w_down):
-    copies = 140
+    moe = jnp.dot(combine[...], returned[...].reshape(768, 384), preferred_element_type=F32)
+    out[...] = (hres[...].astype(F32) + moe).astype(BF16)
+
+
+def on_device(
+    resid, queries, keys, values, w_out, norm_gain, w_gate, w_up, w_down, expert_ids, route_units
+):
+    gain = jnp.broadcast_to(norm_gain.astype(F32)[None], (8, norm_gain.shape[0]))
+    copies = 200
     return pl.pallas_call(
-        experts_kernel,
-        out_shape=jax.ShapeDtypeStruct((8, 96, 384), BF16),
-        in_specs=[pl.BlockSpec(memory_space=pltpu.VMEM)] + [pl.BlockSpec(memory_space=pl.ANY)] * 3,
+        layer_kernel,
+        out_shape=jax.ShapeDtypeStruct((256, 384), BF16),
+        in_specs=[pl.BlockSpec(memory_space=pl.ANY)] * 11,
         out_specs=pl.BlockSpec(memory_space=pltpu.VMEM),
         scratch_shapes=[
+            pltpu.VMEM((256, 384), BF16),
+            pltpu.VMEM((256, 768), BF16),
+            pltpu.VMEM((256, HD), BF16),
+            pltpu.VMEM((256, HD), BF16),
+            pltpu.VMEM((768, 384), BF16),
+            pltpu.VMEM((256, 2), jnp.int32),
+            pltpu.VMEM((256, 2), jnp.int32),
+            pltpu.VMEM((16, 128, HD), BF16),
+            pltpu.VMEM((16, 128, HD), BF16),
+            pltpu.VMEM((16, 8, 384), F32),
+            pltpu.VMEM((256, 768), BF16),
+            pltpu.VMEM((256, 768), BF16),
+            pltpu.VMEM((256, 384), BF16),
+            pltpu.VMEM((8, 96, 384), BF16),
             pltpu.VMEM((4, 4, 8, 96, 384), BF16),
             pltpu.VMEM((6144, 512), BF16),
             pltpu.VMEM((6144, 512), BF16),
             pltpu.VMEM((512, 6144), BF16),
+            pltpu.VMEM((2, 384, 128), F32),
             pltpu.VMEM((2, 384, 512), F32),
             pltpu.VMEM((2, 384, 512), F32),
             pltpu.VMEM((8, 96, 512), BF16),
@@ -548,50 +601,17 @@
             pltpu.VMEM((2, 5, 2, 4, 96, 384), BF16),
             pltpu.VMEM((8, 96, 384), BF16),
             pltpu.VMEM((8, 96, 384), BF16),
-            pltpu.SemaphoreType.DMA((3,)),
+            pltpu.SemaphoreType.DMA((11,)),
             pltpu.SemaphoreType.DMA((copies,)),
             pltpu.SemaphoreType.DMA((copies,)),
         ],
         compiler_params=pltpu.CompilerParams(
-            collective_id=1, has_side_effects=True, vmem_limit_bytes=64 * 1024 * 1024 - 128 * 1024
+            collective_id=0, has_side_effects=True, vmem_limit_bytes=64 * 1024 * 1024 - 128 * 1024
         ),
-        name="experts",
-    )(slots, w_gate, w_up, w_down)
-
-
-def on_device(
-    resid, queries, keys, values, w_out, norm_gain, w_gate, w_up, w_down, expert_ids, route_units
-):
-    tp_size = lax.axis_size(TP)
-    tok_rows = queries.shape[0]
-    feat_dev = resid.shape[1]
-    capacity = 3 * tok_rows // tp_size
-    hres, squares = attention(queries, keys, values, w_out, resid)
-    hfloat = hres.astype(jnp.float32)
-    square_total = squares[0][:, None]
-    normed = (hfloat * lax.rsqrt(square_total / D + 1e-05) * norm_gain.astype(jnp.float32)).astype(
-        jnp.bfloat16
+        name="layer",
+    )(
+        resid, queries, keys, values, w_out, gain, w_gate[0], w_up[0], w_down[0], expert_ids, route_units
     )
-    onehot = (expert_ids[..., None] == jnp.arange(tp_size, dtype=jnp.int32)).astype(jnp.int32)
-    per_token = jnp.sum(onehot, axis=1)
-    earlier = jnp.cumsum(per_token, axis=0) - per_token
-    slot = jnp.sum(onehot * earlier[:, None, :], axis=-1)
-    codes = expert_ids * capacity + slot
-    slot_ids = jnp.arange(tp_size * capacity, dtype=jnp.int32)
-    picks = (
-        (slot_ids[:, None] == codes[None, :, 0]) | (slot_ids[:, None] == codes[None, :, 1])
-    ).astype(jnp.bfloat16)
-    dispatched = jnp.dot(picks, normed, preferred_element_type=jnp.float32).astype(jnp.bfloat16)
-    returned = experts(dispatched.reshape(tp_size, capacity, feat_dev), w_gate[0], w_up[0], w_down[0])
-    units = route_units.astype(jnp.float32)
-    weights = (units / jnp.sum(units, axis=-1, keepdims=True)).astype(jnp.bfloat16)
-    combine = jnp.where(slot_ids[None, :] == codes[:, 0:1], weights[:, 0:1], 0.0) + jnp.where(
-        slot_ids[None, :] == codes[:, 1:2], weights[:, 1:2], 0.0
-    )
-    moe = jnp.dot(
-        combine, returned.reshape(tp_size * capacity, feat_dev), preferred_element_type=jnp.float32
-    )
-    return (hfloat + moe).astype(jnp.bfloat16)
 
 
 def solution(mesh):

time: 217 us -> 201 us (0.926)
  Pallas kernels: 204 us -> 195 us
  matrix products: 3.56 us -> 0 us
  other arithmetic: 3.53 us -> 0 us
    pallas_call x2 -> x1, Pallas kernels: 204 us -> 195 us  [on_device(): pl.pallas_call(layer_kernel, out_shape=jax.ShapeDtypeStruct((256, 384), B...]
    dot_general x2 -> x0, matrix products: 3.56 us -> none  [the longest x1 2.3 us: on_device(): jnp.dot(combine, returned.reshape(tp_size * capacity, feat_dev), preferre...]
    unnamed x14 -> x3, local copies, waits for them, and re-layouts: 4.67 us -> 4.55 us
where the time goes in v4:
time: 201 us
  Pallas kernels  195 us (97%)
  local copies, waits for them, and re-layouts  5.83 us (3%)
    pallas_call x1, Pallas kernels, on_device(): pl.pallas_call(layer_kernel, out_shape=jax.ShapeDtypeStruct((256, 384), B...  195 us
    unnamed x3, local copies, waits for them, and re-layouts  4.55 us

profile of v4, /device:TPU:1, one launch (start us, length us, event | category | flops | bytes accessed | tf_op | source)
XLA Modules:
  0.0 201.3 jit_solution(15375907350239687904)
XLA Ops:
  0.0 1.3 broadcast_in_dim.2.gain_hbm
  1.3 1.5 copy.12.ids_hbm
  2.8 1.5 copy.13.units_hbm
  4.2 195.5 %layer.1 = bf16[256,384]{1,0:T(8,128)(2,1)} custom-call(bf16[256,384]{1,0:T(8,128)(2,1)} %resid_hbm.1, bf16[256,768]{1,0:T(8,128)(2,1)} %queries_hbm.1, bf16[256,128]{1,0:T(8,128)(2,1)} %keys_hbm.1, bf16[256,128]{1,0:T(8,128)(2,1)} %values_hbm.1, bf16[768,384]{1,0:T(8,128)(2,1)} %w_out_hbm.1, f32[8,384]{1,0:T(8,128)} %broadcast_in_dim.2.gain_hbm, ...), custom_call_target="tpu_custom_call" | custom-call | tf_op jit(solution)/shard_map/layer/pallas_call | solution.py:571
  199.7 1.6 copy.15

commit v5 on v4

--- a/solution.py
+++ b/solution.py
@@ -46,6 +46,10 @@
         other = lax.rem(self.member + step, 16)
         return {"y": other // 4, "core": lax.rem(other // 2, 2), "zl": lax.rem(other, 2)}
 
+    def ctx_peer(self, step):
+        other = lax.rem(self.ctx + step, 8)
+        return {"zh": other // 4, "x": lax.rem(other, 4)}
+
     def mirror(self):
         return {"zh": self.tp // 4, "x": lax.rem(self.tp, 4), "y": self.ctx // 2, "core": lax.rem(self.ctx, 2)}
 
@@ -85,96 +89,115 @@
         self.open = []
 
 
-GATHER_COPIES = 40
-
-
-def plane_gather(place, link, piece, first=0, ready=None, seen=None, busy=None):
-    here = (place.x, place.z)
-
-    def block(part, along_f, along_s, half=None):
-        f, s = (here[0], here[1]) if part == 0 else (here[1], here[0])
-        f, s = wrapped(f + along_f), wrapped(s + along_s)
-        return piece(f, s, part, half) if part == 0 else piece(s, f, part, half)
-
-    def f_axis(part):
-        return "xz"[part]
-
-    def s_axis(part):
-        return "zx"[part]
-
-    def number(part, kind, g, direction):
-        base = {"near": 0, "far": 2, "near2": 4, "far2": 12}[kind]
-        return first + part * 20 + base + (FAR_FIRST.index(g) * 2 if kind in ("near2", "far2") else 0) + direction
-
-    def pass_on(part, g):
-        ref = block(part, g, 0)
-        for direction, step in ((0, 1), (1, -1)):
-            link.send(number(part, "near2", g, direction), ref, ref, place.beside(s_axis(part), step))
-
-    for part in (0, 1):
+WAYS = ((0, 1), (1, -1))
+
+
+class Gather:
+    def __init__(self, place, link, piece, first):
+        self.place, self.link, self.piece, self.first = place, link, piece, first
+
+    def block(self, part, along_f, along_s, half=None):
+        x, z = (along_f, along_s) if part == 0 else (along_s, along_f)
+        return self.piece(wrapped(self.place.x + x), wrapped(self.place.z + z), part, half)
+
+    def number(self, part, kind, direction, g=2):
+        return self.first + part * 20 + {"near": 0, "far": 2, "near2": 4, "far2": 12}[kind] + (
+            FAR_FIRST.index(g) * 2 + direction
+        )
+
+    def near(self, part):
+        ref = self.block(part, 0, 0)
+        for direction, step in WAYS:
+            device = self.place.beside("xz"[part], step)
+            self.link.send(self.number(part, "near", direction), ref, ref, device)
+
+    def far(self, part):
+        for direction, step in WAYS:
+            back = self.place.beside("xz"[part], -step)
+            self.link.arrived(self.number(part, "near", direction), self.block(part, -step, 0), back)
+            ref = self.block(part, -step, 0, direction)
+            device = self.place.beside("xz"[part], step)
+            self.link.send(self.number(part, "far", direction), ref, ref, device)
+
+    def far_done(self, part):
+        for direction, step in WAYS:
+            back = self.place.beside("xz"[part], -step)
+            self.link.arrived(self.number(part, "far", direction), self.block(part, 2, 0, direction), back)
+
+    def near2(self, part, g):
+        ref = self.block(part, g, 0)
+        for direction, step in WAYS:
+            device = self.place.beside("zx"[part], step)
+            self.link.send(self.number(part, "near2", direction, g), ref, ref, device)
+
+    def far2(self, part, g):
+        for direction, step in WAYS:
+            back = self.place.beside("zx"[part], -step)
+            self.link.arrived(self.number(part, "near2", direction, g), self.block(part, g, -step), back)
+            ref = self.block(part, g, -step, direction)
+            device = self.place.beside("zx"[part], step)
+            self.link.send(self.number(part, "far2", direction, g), ref, ref, device)
+
+    def far2_done(self, part, g):
+        for direction, step in WAYS:
+            back = self.place.beside("zx"[part], -step)
+            number = self.number(part, "far2", direction, g)
+            self.link.arrived(number, self.block(part, g, 2, direction), back)
+
+
+def plane_gather(gather, ready=None, busy=None, seen=None):
+    both = (0, 1)
+    for part in both:
         if ready is not None:
             ready(part)
-        ref = block(part, 0, 0)
-        for direction, step in ((0, 1), (1, -1)):
-            link.send(number(part, "near", 0, direction), ref, ref, place.beside(f_axis(part), step))
+        gather.near(part)
         if ready is not None:
-            pass_on(part, 0)
+            gather.near2(part, 0)
     if ready is None:
-        for part in (0, 1):
-            pass_on(part, 0)
+        for part in both:
+            gather.near2(part, 0)
     if busy is not None:
         busy()
-    for part in (0, 1):
-        for direction, step in ((0, 1), (1, -1)):
-            back = place.beside(f_axis(part), -step)
-            link.arrived(number(part, "near", 0, direction), block(part, -step, 0), back)
-            ref = block(part, -step, 0, direction)
-            link.send(number(part, "far", 0, direction), ref, ref, place.beside(f_axis(part), step))
-    for part in (0, 1):
-        pass_on(part, -1)
-        pass_on(part, 1)
-
-    def relay(part, g):
-        for direction, step in ((0, 1), (1, -1)):
-            back = place.beside(s_axis(part), -step)
-            link.arrived(number(part, "near2", g, direction), block(part, g, -step), back)
-            ref = block(part, g, -step, direction)
-            link.send(number(part, "far2", g, direction), ref, ref, place.beside(s_axis(part), step))
-
-    def last(g):
-        for part in (0, 1):
-            for direction, step in ((0, 1), (1, -1)):
-                back = place.beside(s_axis(part), -step)
-                link.arrived(number(part, "far2", g, direction), block(part, g, 2, direction), back)
-
-    def use(part, along_z):
-        if seen is not None:
-            seen(part, along_z)
-
-    for part in (0, 1):
-        relay(part, 0)
-    for part in (0, 1):
-        for direction, step in ((0, 1), (1, -1)):
-            back = place.beside(f_axis(part), -step)
-            link.arrived(number(part, "far", 0, direction), block(part, 2, 0, direction), back)
-        pass_on(part, 2)
-    use(0, 0)
+    for part in both:
+        gather.far(part)
+    for part in both:
+        gather.near2(part, -1)
+        gather.near2(part, 1)
+    for part in both:
+        gather.far2(part, 0)
+    for part in both:
+        gather.far_done(part)
+        gather.near2(part, 2)
+    seen = seen or (lambda *_: None)
+    seen(0, 0)
     for g in (-1, 1):
-        for part in (0, 1):
-            relay(part, g)
-    last(0)
-    use(1, 0)
-    for part in (0, 1):
-        relay(part, 2)
-    use(0, -1)
-    use(0, 1)
+        for part in both:
+            gather.far2(part, g)
+    for part in both:
+        gather.far2_done(part, 0)
+    seen(1, 0)
+    seen(2, 0)
+    for part in both:
+        gather.far2(part, 2)
+    seen(0, -1)
+    seen(0, 1)
+    seen(2, 1)
     for g in (-1, 1):
-        last(g)
-    use(1, -1)
-    use(1, 1)
-    last(2)
-    use(0, 2)
-    use(1, 2)
+        for part in both:
+            gather.far2_done(part, g)
+    seen(1, -1)
+    seen(1, 1)
+    seen(2, -1)
+    for part in both:
+        gather.far2_done(part, 2)
+    seen(0, 2)
+    seen(1, 2)
+    seen(2, 2)
+
+
+def picked(tile):
+    slot_ids = lax.broadcasted_iota(jnp.int32, (768, 256), 0).astype(F32)
+    return slot_ids == tile[0:1, :], slot_ids == tile[1:2, :]
 
 
 def layer_kernel(
@@ -199,12 +222,15 @@
     units,
     all_keys,
     all_values,
+    gain,
     gains,
-    picks,
+    codes,
     combine,
     hres,
     slots,
     rows,
+    tokens,
+    token_rows,
     gate_w,
     up_w,
     down_w,
@@ -228,7 +254,7 @@
         (keys_hbm, keys),
         (values_hbm, values),
         (queries_hbm, queries),
-        (gain_hbm, gains.at[place.member]),
+        (gain_hbm, gain),
         (ids_hbm, ids),
         (units_hbm, units),
         (w_out_hbm, w_out),
@@ -243,7 +269,8 @@
     barrier = pltpu.get_barrier_semaphore()
     diagonal = place.ctx == place.tp
     members = [place.member_peer(step) for step in range(1, 16)]
-    greeted = place.greet(members)
+    ctx_peers = [place.ctx_peer(step) for step in range(1, 8)]
+    greeted = place.greet(members + ctx_peers)
     for load in loads[:2]:
         load.wait()
 
@@ -272,32 +299,38 @@
 
     def route():
         loads[3].wait()
+        gains[place.member] = jnp.broadcast_to(gain[...].astype(F32).reshape(1, 384), (8, 384))
         for step in range(1, 16):
             ref = gains.at[place.member]
             link.send(88 + step, ref, ref, members[step - 1])
         loads[4].wait()
         loads[5].wait()
-        lanes = lax.broadcasted_iota(jnp.int32, (256, 128), 1)
-        named = [ids[:, k : k + 1] == lanes for k in range(2)]
-        tokens = jnp.where(named[0] | named[1], 1.0, 0.0).astype(BF16)
+        line = lax.broadcasted_iota(jnp.int32, (8, 256), 0)
+        numbers = ids[...]
+        named = [line == numbers[k : k + 1, :] for k in range(2)]
+        uses = jnp.where(named[0] | named[1], 1.0, 0.0).astype(BF16)
         row = lax.broadcasted_iota(jnp.int32, (256, 256), 0)
         column = lax.broadcasted_iota(jnp.int32, (256, 256), 1)
-        before = jnp.where(column < row, 1.0, 0.0).astype(BF16)
-        earlier = jnp.dot(before, tokens, preferred_element_type=F32)
+        before = jnp.where(row < column, 1.0, 0.0).astype(BF16)
+        earlier = jnp.dot(uses, before, preferred_element_type=F32)
         amounts = units[...].astype(F32)
-        weights = (amounts / jnp.sum(amounts, axis=1, keepdims=True)).astype(BF16).astype(F32)
-        slot_ids = lax.broadcasted_iota(jnp.int32, (256, 768), 1).astype(F32)
-        hits = []
+        total = amounts[0:1, :] + amounts[1:2, :]
+        tile = jnp.zeros((8, 256), F32)
         for k in range(2):
-            slot = jnp.sum(jnp.where(named[k], earlier, 0.0), axis=1, keepdims=True)
-            code = ids[:, k : k + 1].astype(F32) * 96.0 + slot
-            hits.append(slot_ids == code)
-        picks[...] = jnp.where(hits[0] | hits[1], 1.0, 0.0).astype(BF16)
+            slot = jnp.sum(jnp.where(named[k], earlier, 0.0), axis=0, keepdims=True)
+            code = numbers[k : k + 1, :].astype(F32) * 96.0 + slot
+            weight = (amounts[k : k + 1, :] / total).astype(BF16).astype(F32)
+            tile = jnp.where(line == k, code, jnp.where(line == 2 + k, weight, tile))
+        codes[place.ctx] = tile
+        for step in range(1, 8):
+            ref = codes.at[place.ctx]
+            link.send(200 + step, ref, ref, ctx_peers[step - 1])
+        hits = picked(tile)
         combine[...] = (
-            jnp.where(hits[0], weights[:, 0:1], 0.0) + jnp.where(hits[1], weights[:, 1:2], 0.0)
+            jnp.where(hits[0], tile[2:3, :], 0.0) + jnp.where(hits[1], tile[3:4, :], 0.0)
         ).astype(BF16)
 
-    plane_gather(place, link, key_block, busy=route)
+    plane_gather(Gather(place, link, key_block, 0), busy=route)
     loads[2].wait()
 
     def attn_rows(part, block, start, count):
@@ -329,7 +362,7 @@
             return gate_w.at[attn_rows(part, at(x, z), 0, 128)]
         return gate_w.at[attn_rows(part, at(x, z), half * 64, 64)]
 
-    plane_gather(place, link, attn_block, first=40, ready=attend)
+    plane_gather(Gather(place, link, attn_block, 40), ready=attend)
 
     loads[6].wait()
 
@@ -378,10 +411,19 @@
 
     loads[7].wait()
     hres[...] = (resid[...].astype(F32) + piece(15)[...].astype(F32)).astype(BF16)
-    dispatched = lax.dot_general(
-        picks[...], hres[...], (((0,), (0,)), ((), ())), preferred_element_type=F32
-    ).astype(BF16)
-    slots[...] = dispatched.reshape(8, 96, 384)
+
+    def token_block(x, z, part, half):
+        if half is None:
+            return tokens.at[at(x, z)]
+        return tokens.at[at(x, z), pl.ds(half * 128, 128)]
+
+    flow = Gather(place, link, token_block, 220)
+    tokens[here] = hres[:, 256:384]
+    flow.near(1)
+    flow.near2(1, 0)
+    hits = picked(codes[place.ctx])
+    picks = jnp.where(hits[0] | hits[1], 1.0, 0.0).astype(BF16)
+    slots[...] = jnp.dot(picks, hres[:, 0:256], preferred_element_type=F32).astype(BF16).reshape(8, 96, 256)
 
     base = 104
     for step in range(1, 8):
@@ -395,6 +437,34 @@
 
     pieces.finish()
     loads[10].start()
+    flow.far(1)
+    for step in range(1, 8):
+        source = lax.rem(place.ctx + 8 - step, 8)
+        link.arrived(200 + step, codes.at[source], ctx_peers[7 - step])
+    flow.near2(1, -1)
+    flow.near2(1, 1)
+    flow.far_done(1)
+    flow.near2(1, 2)
+
+    def chosen(x, target):
+        return partial.at[x, pl.ds(0, 2), target, :, pl.ds(0, 256)]
+
+    def send_group(g):
+        x = wrapped(place.x + g)
+        for zh in range(2):
+            ctx = zh * 4 + x
+            hits = picked(codes[ctx])
+            picks = jnp.where(hits[0] | hits[1], 1.0, 0.0).astype(BF16)
+            both = jnp.concatenate([tokens[2 * ctx], tokens[2 * ctx + 1]], axis=1)
+            taken = jnp.dot(picks, both, preferred_element_type=F32).astype(BF16)
+            partial[x, zh, :, :, 0:256] = taken.reshape(8, 96, 256)
+        for step in range(1, 8):
+            target = lax.rem(place.tp + step, 8)
+            number = 208 + FAR_FIRST.index(g) * 8 + step
+            link.send(number, chosen(x, target), token_rows.at[place.tp, x], place.tp_peer(step))
+        token_rows[place.tp, x] = chosen(x, place.tp)[...]
+
+    send_group(0)
     gate_acc[...] = jnp.zeros_like(gate_acc)
     up_acc[...] = jnp.zeros_like(up_acc)
     row_squares[...] = jnp.zeros_like(row_squares)
@@ -410,11 +480,28 @@
             return rows.at[x, z, pl.ds(part * 4, 4)]
         return rows.at[x, z, pl.ds(part * 4 + half * 2, 2)]
 
-    def use_rows(part, along_z):
-        if (part, along_z) == (0, 0):
+    def more_groups():
+        for g in (0, 1, -1, 2):
+            flow.far2(1, g)
+        for g in (0, 1, -1, 2):
+            flow.far2_done(1, g)
+        for g in (1, -1, 2):
+            send_group(g)
+
+    def scaled(value, blocks):
+        value = value.astype(F32)
+        square = value * value
+        squares = square[:, 0:128] + square[:, 128:256]
+        return (value * blocks).astype(BF16), squares
+
+    def use_rows(part, along):
+        if (part, along) == (0, 0):
             loads[9].wait()
             loads[10].wait()
-        z = wrapped(place.z + along_z)
+        if part == 2:
+            use_tokens(along)
+            return
+        z = wrapped(place.z + along)
         zh, e = z // 2, lax.rem(z, 2)
 
         @pl.loop(part * 2, part * 2 + 2)
@@ -423,23 +510,47 @@
             squares = row_squares[zh]
             for i in range(2):
                 t = 2 * pair + i
-                value = rows[:, z, t].reshape(384, 384).astype(F32)
-                lefts.append((value * gains[2 * t + e, 0:1, :]).astype(BF16))
-                square = value * value
-                squares = squares + square[:, 0:128] + square[:, 128:256] + square[:, 256:384]
+                left, more = scaled(rows[:, z, t].reshape(384, 256), gains[2 * t + e, 0:1, 0:256])
+                lefts.append(left)
+                squares = squares + more.reshape(4, 96, 128)
             row_squares[zh] = squares
             left = jnp.concatenate(lefts, axis=1)
-            spans = [pl.ds(pl.multiple_of((4 * pair + 2 * i + e) * 384, 384), 384) for i in range(2)]
+            spans = [pl.ds(pl.multiple_of((4 * pair + 2 * i + e) * 384, 128), 256) for i in range(2)]
             for acc, weights in ((gate_acc, gate_w), (up_acc, up_w)):
                 right = jnp.concatenate([weights[span, :] for span in spans], axis=0)
-                acc[zh] += jnp.dot(left, right, preferred_element_type=F32)
-
-    plane_gather(place, link, block_of_rows, first=112, seen=use_rows)
+                acc[zh] += jnp.dot(left, right, preferred_element_type=F32).reshape(4, 96, 512)
+
+    def use_tokens(g):
+        x = wrapped(place.x + g)
+        for step in range(1, 8):
+            source = lax.rem(place.tp + 8 - step, 8)
+            number = 208 + FAR_FIRST.index(g) * 8 + step
+            link.arrived(number, token_rows.at[source, x], place.tp_peer(8 - step))
+
+        @pl.loop(0, 4)
+        def _(pair):
+            lefts, spans = [], []
+            squares = row_squares[:, x]
+            for i in range(2):
+                t = 2 * pair + i
+                blocks = jnp.concatenate([gains[2 * t + e, 0:1, 256:384] for e in range(2)], axis=1)
+                left, more = scaled(token_rows[t, x].reshape(192, 256), blocks)
+                lefts.append(left)
+                squares = squares + more.reshape(2, 96, 128)
+                spans += [pl.ds(pl.multiple_of((2 * t + e) * 384 + 256, 128), 128) for e in range(2)]
+            row_squares[:, x] = squares
+            left = jnp.concatenate(lefts, axis=1)
+            for acc, weights in ((gate_acc, gate_w), (up_acc, up_w)):
+                right = jnp.concatenate([weights[span, :] for span in spans], axis=0)
+                acc[:, x] += jnp.dot(left, right, preferred_element_type=F32).reshape(2, 96, 512)
+
+    plane_gather(Gather(place, link, block_of_rows, 112), busy=more_groups, seen=use_rows)
+    link.finish()
     for zh in range(2):
-        mean = jnp.sum(row_squares[zh], axis=1, keepdims=True) / D
+        mean = jnp.sum(row_squares[zh].reshape(384, 128), axis=1, keepdims=True) / D
         scale = lax.rsqrt(mean + 1e-05)
-        gate = gate_acc[zh] * scale
-        value = gate / (1.0 + jnp.exp(-gate)) * (up_acc[zh] * scale)
+        gate = gate_acc[zh].reshape(384, 512) * scale
+        value = gate / (1.0 + jnp.exp(-gate)) * (up_acc[zh].reshape(384, 512) * scale)
         hidden[pl.ds(zh * 4, 4)] = value.astype(BF16).reshape(4, 96, 512)
     loads[8].wait()
 
@@ -559,15 +670,19 @@
         source = lax.rem(place.tp + 8 - step, 8)
         link.arrived(base + step, returned.at[source], place.tp_peer(8 - step))
     link.finish()
-    moe = jnp.dot(combine[...], returned[...].reshape(768, 384), preferred_element_type=F32)
+    moe = lax.dot_general(
+        combine[...],
+        returned[...].reshape(768, 384),
+        (((0,), (0,)), ((), ())),
+        preferred_element_type=F32,
+    )
     out[...] = (hres[...].astype(F32) + moe).astype(BF16)
 
 
 def on_device(
     resid, queries, keys, values, w_out, norm_gain, w_gate, w_up, w_down, expert_ids, route_units
 ):
-    gain = jnp.broadcast_to(norm_gain.astype(F32)[None], (8, norm_gain.shape[0]))
-    copies = 200
+    copies = 260
     return pl.pallas_call(
         layer_kernel,
         out_shape=jax.ShapeDtypeStruct((256, 384), BF16),
@@ -579,22 +694,25 @@
             pltpu.VMEM((256, HD), BF16),
             pltpu.VMEM((256, HD), BF16),
             pltpu.VMEM((768, 384), BF16),
-            pltpu.VMEM((256, 2), jnp.int32),
-            pltpu.VMEM((256, 2), jnp.int32),
+            pltpu.VMEM((2, 256), jnp.int32),
+            pltpu.VMEM((2, 256), jnp.int32),
             pltpu.VMEM((16, 128, HD), BF16),
             pltpu.VMEM((16, 128, HD), BF16),
+            pltpu.VMEM((384,), BF16),
             pltpu.VMEM((16, 8, 384), F32),
-            pltpu.VMEM((256, 768), BF16),
-            pltpu.VMEM((256, 768), BF16),
+            pltpu.VMEM((8, 8, 256), F32),
+            pltpu.VMEM((768, 256), BF16),
             pltpu.VMEM((256, 384), BF16),
-            pltpu.VMEM((8, 96, 384), BF16),
-            pltpu.VMEM((4, 4, 8, 96, 384), BF16),
+            pltpu.VMEM((8, 96, 256), BF16),
+            pltpu.VMEM((4, 4, 8, 96, 256), BF16),
+            pltpu.VMEM((16, 256, 128), BF16),
+            pltpu.VMEM((8, 4, 2, 96, 256), BF16),
             pltpu.VMEM((6144, 512), BF16),
             pltpu.VMEM((6144, 512), BF16),
             pltpu.VMEM((512, 6144), BF16),
-            pltpu.VMEM((2, 384, 128), F32),
-            pltpu.VMEM((2, 384, 512), F32),
-            pltpu.VMEM((2, 384, 512), F32),
+            pltpu.VMEM((2, 4, 96, 128), F32),
+            pltpu.VMEM((2, 4, 96, 512), F32),
+            pltpu.VMEM((2, 4, 96, 512), F32),
             pltpu.VMEM((8, 96, 512), BF16),
             pltpu.VMEM((4, 4, 8, 96, 384), BF16),
             pltpu.VMEM((2, 5, 2, 2, 96, 384), BF16),
@@ -610,7 +728,17 @@
         ),
         name="layer",
     )(
-        resid, queries, keys, values, w_out, gain, w_gate[0], w_up[0], w_down[0], expert_ids, route_units
+        resid,
+        queries,
+        keys,
+        values,
+        w_out,
+        norm_gain,
+        w_gate[0],
+        w_up[0],
+        w_down[0],
+        expert_ids.T,
+        route_units.T,
     )
 
 

time: 201 us -> 190 us (0.945)
  Pallas kernels: 195 us -> 189 us
  local copies, waits for them, and re-layouts: 5.83 us -> 1.62 us
    pallas_call x1, Pallas kernels: 195 us -> 189 us  [on_device(): pl.pallas_call(layer_kernel, out_shape=jax.ShapeDtypeStruct((256, 384), B...]
    unnamed x3 -> x1, local copies, waits for them, and re-layouts: 4.55 us -> 1.62 us
where the time goes in v5:
time: 190 us
  Pallas kernels  189 us (99%)
    pallas_call x1, Pallas kernels, on_device(): pl.pallas_call(layer_kernel, out_shape=jax.ShapeDtypeStruct((256, 384), B...  189 us

profile of v5, /device:TPU:1, one launch (start us, length us, event | category | flops | bytes accessed | tf_op | source)
XLA Modules:
  0.0 190.3 jit_solution(9540953166684489656)
XLA Ops:
  0.0 188.7 %layer.1 = bf16[256,384]{1,0:T(8,128)(2,1)} custom-call(bf16[256,384]{1,0:T(8,128)(2,1)} %resid_hbm.1, bf16[256,768]{1,0:T(8,128)(2,1)} %queries_hbm.1, bf16[256,128]{1,0:T(8,128)(2,1)} %keys_hbm.1, bf16[256,128]{1,0:T(8,128)(2,1)} %values_hbm.1, bf16[768,384]{1,0:T(8,128)(2,1)} %w_out_hbm.1, bf16[384]{0:T(512)(128)(2,1)} %gain_hbm.1, ...), custom_call_target="tpu_custom_call" | custom-call | tf_op jit(solution)/shard_map/layer/pallas_call | solution.py:686
  188.7 1.6 copy.13

commit v6 on v5

--- a/solution.py
+++ b/solution.py
@@ -145,7 +145,7 @@
             self.link.arrived(number, self.block(part, g, 2, direction), back)
 
 
-def plane_gather(gather, ready=None, busy=None, seen=None):
+def plane_gather(gather, ready=None, busy=None, later=None, seen=None):
     both = (0, 1)
     for part in both:
         if ready is not None:
@@ -163,6 +163,8 @@
     for part in both:
         gather.near2(part, -1)
         gather.near2(part, 1)
+    if later is not None:
+        later()
     for part in both:
         gather.far2(part, 0)
     for part in both:
@@ -241,6 +243,11 @@
     partial,
     got_half,
     got_part,
+    back_rows,
+    x_half,
+    x_part,
+    z_half,
+    z_part,
     result,
     returned,
     load_sem,
@@ -413,12 +420,14 @@
     hres[...] = (resid[...].astype(F32) + piece(15)[...].astype(F32)).astype(BF16)
 
     def token_block(x, z, part, half):
+        where = z // 2, 2 * x + lax.rem(z, 2)
         if half is None:
-            return tokens.at[at(x, z)]
-        return tokens.at[at(x, z), pl.ds(half * 128, 128)]
+            return tokens.at[where]
+        return tokens.at[(*where, pl.ds(half * 128, 128))]
 
     flow = Gather(place, link, token_block, 220)
-    tokens[here] = hres[:, 256:384]
+    own = place.z // 2, 2 * place.x + place.zl
+    tokens[own] = hres[:, 256:384]
     flow.near(1)
     flow.near2(1, 0)
     hits = picked(codes[place.ctx])
@@ -443,11 +452,9 @@
         link.arrived(200 + step, codes.at[source], ctx_peers[7 - step])
     flow.near2(1, -1)
     flow.near2(1, 1)
-    flow.far_done(1)
-    flow.near2(1, 2)
 
     def chosen(x, target):
-        return partial.at[x, pl.ds(0, 2), target, :, pl.ds(0, 256)]
+        return partial.at[x, pl.ds(0, 2), target]
 
     def send_group(g):
         x = wrapped(place.x + g)
@@ -455,19 +462,15 @@
             ctx = zh * 4 + x
             hits = picked(codes[ctx])
             picks = jnp.where(hits[0] | hits[1], 1.0, 0.0).astype(BF16)
-            both = jnp.concatenate([tokens[2 * ctx], tokens[2 * ctx + 1]], axis=1)
+            both = jnp.concatenate([tokens[zh, 2 * x + e] for e in range(2)], axis=1)
             taken = jnp.dot(picks, both, preferred_element_type=F32).astype(BF16)
-            partial[x, zh, :, :, 0:256] = taken.reshape(8, 96, 256)
+            partial[x, zh] = taken.reshape(8, 96, 256)
         for step in range(1, 8):
             target = lax.rem(place.tp + step, 8)
             number = 208 + FAR_FIRST.index(g) * 8 + step
             link.send(number, chosen(x, target), token_rows.at[place.tp, x], place.tp_peer(step))
         token_rows[place.tp, x] = chosen(x, place.tp)[...]
 
-    send_group(0)
-    gate_acc[...] = jnp.zeros_like(gate_acc)
-    up_acc[...] = jnp.zeros_like(up_acc)
-    row_squares[...] = jnp.zeros_like(row_squares)
     for step in range(1, 16):
         source = lax.rem(place.member + 16 - step, 16)
         link.arrived(88 + step, gains.at[source], members[15 - step])
@@ -480,13 +483,21 @@
             return rows.at[x, z, pl.ds(part * 4, 4)]
         return rows.at[x, z, pl.ds(part * 4 + half * 2, 2)]
 
-    def more_groups():
+    def first_group():
+        flow.far_done(1)
+        flow.near2(1, 2)
+        send_group(0)
         for g in (0, 1, -1, 2):
             flow.far2(1, g)
+
+    def more_groups():
         for g in (0, 1, -1, 2):
             flow.far2_done(1, g)
         for g in (1, -1, 2):
             send_group(g)
+        gate_acc[...] = jnp.zeros_like(gate_acc)
+        up_acc[...] = jnp.zeros_like(up_acc)
+        row_squares[...] = jnp.zeros_like(row_squares)
 
     def scaled(value, blocks):
         value = value.astype(F32)
@@ -544,7 +555,7 @@
                 right = jnp.concatenate([weights[span, :] for span in spans], axis=0)
                 acc[:, x] += jnp.dot(left, right, preferred_element_type=F32).reshape(2, 96, 512)
 
-    plane_gather(Gather(place, link, block_of_rows, 112), busy=more_groups, seen=use_rows)
+    plane_gather(Gather(place, link, block_of_rows, 112), busy=first_group, later=more_groups, seen=use_rows)
     link.finish()
     for zh in range(2):
         mean = jnp.sum(row_squares[zh].reshape(384, 128), axis=1, keepdims=True) / D
@@ -561,11 +572,13 @@
 
             @pl.loop(0, 4)
             def _(t):
-                right = down_w[:, pl.ds(pl.multiple_of(t * 768, 768), 768)]
+                right = jnp.concatenate(
+                    [down_w[:, pl.ds(pl.multiple_of((2 * t + e) * 384, 128), 256)] for e in range(2)], axis=1
+                )
                 both = jnp.dot(left, right, preferred_element_type=F32).astype(BF16)
                 for zh in range(2):
                     for e in range(2):
-                        partial[x, zh * 2 + e, t] = both[zh * 96 : zh * 96 + 96, e * 384 : e * 384 + 384]
+                        partial[x, zh * 2 + e, t] = both[zh * 96 : zh * 96 + 96, e * 256 : e * 256 + 256]
         else:
             z = wrapped(place.z + g)
             left = hidden[pl.ds((z // 2) * 4, 4)].reshape(384, 512)
@@ -573,19 +586,49 @@
             @pl.loop(4, 8)
             def _(t):
                 start = (2 * t + lax.rem(z, 2)) * 384
-                right = down_w[:, pl.ds(pl.multiple_of(start, 384), 384)]
+                right = down_w[:, pl.ds(pl.multiple_of(start, 128), 256)]
                 both = jnp.dot(left, right, preferred_element_type=F32).astype(BF16)
-                partial[:, z, t] = both.reshape(4, 96, 384)
-
-    def block(part, along_f, along_s):
-        x, z = (along_f, along_s) if part == 0 else (along_s, along_f)
-        return wrapped(place.x + x), wrapped(place.z + z)
-
-    def half_of(where, part, half):
-        return partial.at[where[0], where[1], pl.ds(part * 4 + half * 2, 2)]
-
-    def part_of(where, part):
-        return partial.at[where[0], where[1], pl.ds(part * 4, 4)]
+                partial[:, z, t] = both.reshape(4, 96, 256)
+
+    def send_back(g):
+        x = wrapped(place.x + g)
+        left = jnp.concatenate([hidden[x], hidden[4 + x]], axis=0)
+
+        @pl.loop(0, 8)
+        def _(t):
+            right = jnp.concatenate(
+                [down_w[:, pl.ds(pl.multiple_of((2 * t + e) * 384 + 256, 128), 128)] for e in range(2)],
+                axis=1,
+            )
+            both = jnp.dot(left, right, preferred_element_type=F32).astype(BF16)
+            token_rows[t, x] = both.reshape(2, 96, 256)
+
+        for step in range(1, 8):
+            target = lax.rem(place.tp + step, 8)
+            number = 260 + FAR_FIRST.index(g) * 8 + step
+            link.send(number, token_rows.at[target, x], back_rows.at[place.tp, x], place.tp_peer(step))
+        back_rows[place.tp, x] = token_rows[place.tp, x]
+
+    def weigh(g):
+        x = wrapped(place.x + g)
+        for step in range(1, 8):
+            source = lax.rem(place.tp + 8 - step, 8)
+            number = 260 + FAR_FIRST.index(g) * 8 + step
+            link.arrived(number, back_rows.at[source, x], place.tp_peer(8 - step))
+        for zh in range(2):
+            tile = codes[zh * 4 + x]
+            hits = picked(tile)
+            shares = (
+                jnp.where(hits[0], tile[2:3, :], 0.0) + jnp.where(hits[1], tile[3:4, :], 0.0)
+            ).astype(BF16)
+            total = lax.dot_general(
+                shares,
+                back_rows[:, x, zh].reshape(768, 256),
+                (((0,), (0,)), ((), ())),
+                preferred_element_type=F32,
+            ).astype(BF16)
+            for e in range(2):
+                tokens[zh, 2 * x + e] = total[:, e * 128 : e * 128 + 128]
 
     def add(target, *sources):
         total = target[...].astype(F32)
@@ -594,71 +637,104 @@
         target[...] = total.astype(BF16)
 
     class Ring:
-        def __init__(self, part, stage, axis, at):
-            self.part, self.stage, self.axis, self.at = part, stage, axis, at
-            self.number = 152 + (part * 5 + stage) * 4
+        def __init__(self, number, axis, whole, half, got_half, got_part):
+            self.number, self.axis, self.whole, self.half = number, axis, whole, half
+            self.got_half, self.got_part = got_half, got_part
 
         def far(self):
-            for direction, step in ((0, 1), (1, -1)):
+            for direction, step in WAYS:
                 link.send(
                     self.number + direction,
-                    half_of(self.at(2), self.part, direction),
-                    got_half.at[self.part, self.stage, direction],
+                    self.half(2, direction),
+                    self.got_half.at[direction],
                     place.beside(self.axis, step),
                 )
 
         def near(self):
-            for direction, step in ((0, 1), (1, -1)):
-                got = got_half.at[self.part, self.stage, direction]
+            for direction, step in WAYS:
+                got = self.got_half.at[direction]
                 link.arrived(self.number + direction, got, place.beside(self.axis, -step))
-                add(half_of(self.at(step), self.part, direction), got)
+                add(self.half(step, direction), got)
                 link.send(
                     self.number + 2 + direction,
-                    part_of(self.at(step), self.part),
-                    got_part.at[self.part, self.stage, direction],
+                    self.whole(step),
+                    self.got_part.at[direction],
                     place.beside(self.axis, step),
                 )
 
         def receive(self):
-            gots = []
-            for direction, step in ((0, 1), (1, -1)):
-                got = got_part.at[self.part, self.stage, direction]
+            for direction, step in WAYS:
+                got = self.got_part.at[direction]
                 link.arrived(self.number + 2 + direction, got, place.beside(self.axis, -step))
-                gots.append(got)
-            return gots
+            return [self.got_part.at[direction] for direction in range(2)]
 
         def end(self):
-            add(part_of(self.at(0), self.part), *self.receive())
+            add(self.whole(0), *self.receive())
+
+    def slot_ring(part, stage, axis, at):
+        def whole(step):
+            x, z = at(step)
+            return partial.at[x, z, pl.ds(part * 4, 4)]
+
+        def half(step, direction):
+            x, z = at(step)
+            return partial.at[x, z, pl.ds(part * 4 + direction * 2, 2)]
+
+        number = 152 + (part * 5 + stage) * 4
+        return Ring(number, axis, whole, half, got_half.at[part, stage], got_part.at[part, stage])
+
+    def spot(part, along_f, along_s):
+        x, z = (along_f, along_s) if part == 0 else (along_s, along_f)
+        return wrapped(place.x + x), wrapped(place.z + z)
 
     outer = [
         {
-            g: Ring(part, FAR_FIRST.index(g), "zx"[part], lambda step, part=part, g=g: block(part, g, step))
+            g: slot_ring(
+                part, FAR_FIRST.index(g), "zx"[part], lambda step, part=part, g=g: spot(part, g, step)
+            )
             for g in FAR_FIRST
         }
         for part in (0, 1)
     ]
-    inner = [Ring(part, 4, "xz"[part], lambda step, part=part: block(part, step, 0)) for part in (0, 1)]
+    inner = [slot_ring(part, 4, "xz"[part], lambda step, part=part: spot(part, step, 0)) for part in (0, 1)]
+
+    def column(step, rows=slice(None)):
+        return tokens.at[:, pl.ds(2 * wrapped(place.x + step), 2), rows]
+
+    def cell(step, rows=slice(None)):
+        z = wrapped(place.z + step)
+        return tokens.at[z // 2, 2 * place.x + lax.rem(z, 2), rows]
+
+    over_x = Ring(292, "x", column, lambda step, d: column(step, pl.ds(d * 128, 128)), x_half, x_part)
+    over_z = Ring(296, "z", cell, lambda step, d: cell(step, pl.ds(d * 128, 128)), z_half, z_part)
+
     for g in FAR_FIRST:
+        send_back(g)
         for part in (0, 1):
             compute(part, g)
             outer[part][g].far()
     for g in (2, 1, -1):
         for part in (0, 1):
             outer[part][g].near()
+    weigh(2)
+    over_x.far()
     for part in (0, 1):
         outer[part][2].end()
         inner[part].far()
     for part in (0, 1):
         outer[part][0].near()
+    weigh(1)
     for part in (0, 1):
         outer[part][1].end()
         outer[part][-1].end()
         inner[part].near()
+    weigh(-1)
+    over_x.near()
     base = 192
     for part in (0, 1):
         outer[part][0].end()
         gots = inner[part].receive()
-        total = part_of(inner[part].at(0), part)[...].astype(F32)
+        total = inner[part].whole(0)[...].astype(F32)
         for got in gots:
             total = total + got[...].astype(F32)
         result[pl.ds(part * 4, 4)] = total.astype(BF16)
@@ -666,23 +742,31 @@
         target = lax.rem(place.tp + step, 8)
         link.send(base + step, result.at[target], returned.at[place.tp], place.tp_peer(step))
     returned[place.tp] = result[place.tp]
+    weigh(0)
+    over_x.end()
+    over_z.far()
+    over_z.near()
     for step in range(1, 8):
         source = lax.rem(place.tp + 8 - step, 8)
         link.arrived(base + step, returned.at[source], place.tp_peer(8 - step))
-    link.finish()
     moe = lax.dot_general(
         combine[...],
-        returned[...].reshape(768, 384),
+        returned[...].reshape(768, 256),
         (((0,), (0,)), ((), ())),
         preferred_element_type=F32,
     )
-    out[...] = (hres[...].astype(F32) + moe).astype(BF16)
+    out[:, 0:256] = (hres[:, 0:256].astype(F32) + moe).astype(BF16)
+    total = over_z.whole(0)[...].astype(F32)
+    for got in over_z.receive():
+        total = total + got[...].astype(F32)
+    out[:, 256:384] = (hres[:, 256:384].astype(F32) + total).astype(BF16)
+    link.finish()
 
 
 def on_device(
     resid, queries, keys, values, w_out, norm_gain, w_gate, w_up, w_down, expert_ids, route_units
 ):
-    copies = 260
+    copies = 300
     return pl.pallas_call(
         layer_kernel,
         out_shape=jax.ShapeDtypeStruct((256, 384), BF16),
@@ -705,7 +789,7 @@
             pltpu.VMEM((256, 384), BF16),
             pltpu.VMEM((8, 96, 256), BF16),
             pltpu.VMEM((4, 4, 8, 96, 256), BF16),
-            pltpu.VMEM((16, 256, 128), BF16),
+            pltpu.VMEM((2, 8, 256, 128), BF16),
             pltpu.VMEM((8, 4, 2, 96, 256), BF16),
             pltpu.VMEM((6144, 512), BF16),
             pltpu.VMEM((6144, 512), BF16),
@@ -714,11 +798,16 @@
             pltpu.VMEM((2, 4, 96, 512), F32),
             pltpu.VMEM((2, 4, 96, 512), F32),
             pltpu.VMEM((8, 96, 512), BF16),
-            pltpu.VMEM((4, 4, 8, 96, 384), BF16),
-            pltpu.VMEM((2, 5, 2, 2, 96, 384), BF16),
-            pltpu.VMEM((2, 5, 2, 4, 96, 384), BF16),
-            pltpu.VMEM((8, 96, 384), BF16),
-            pltpu.VMEM((8, 96, 384), BF16),
+            pltpu.VMEM((4, 4, 8, 96, 256), BF16),
+            pltpu.VMEM((2, 5, 2, 2, 96, 256), BF16),
+            pltpu.VMEM((2, 5, 2, 4, 96, 256), BF16),
+            pltpu.VMEM((8, 4, 2, 96, 256), BF16),
+            pltpu.VMEM((2, 2, 2, 128, 128), BF16),
+            pltpu.VMEM((2, 2, 2, 256, 128), BF16),
+            pltpu.VMEM((2, 128, 128), BF16),
+            pltpu.VMEM((2, 256, 128), BF16),
+            pltpu.VMEM((8, 96, 256), BF16),
+            pltpu.VMEM((8, 96, 256), BF16),
             pltpu.SemaphoreType.DMA((11,)),
             pltpu.SemaphoreType.DMA((copies,)),
             pltpu.SemaphoreType.DMA((copies,)),

time: 190 us -> 187 us (0.984); the launches traced: 190 us -> 185 us
  Pallas kernels: 189 us -> 183 us
    pallas_call x1, Pallas kernels: 189 us -> 183 us  [on_device(): pl.pallas_call(layer_kernel, out_shape=jax.ShapeDtypeStruct((256, 384), B...]
where the time goes in v6:
time: 187 us; the launch traced here: 185 us
  Pallas kernels  183 us (98%)
    pallas_call x1, Pallas kernels, on_device(): pl.pallas_call(layer_kernel, out_shape=jax.ShapeDtypeStruct((256, 384), B...  183 us

profile of v6, /device:TPU:1, one launch (start us, length us, event | category | flops | bytes accessed | tf_op | source)
XLA Modules:
  0.0 184.5 jit_solution(2295898926946354121)
XLA Ops:
  0.0 182.9 %layer.1 = bf16[256,384]{1,0:T(8,128)(2,1)} custom-call(bf16[256,384]{1,0:T(8,128)(2,1)} %resid_hbm.1, bf16[256,768]{1,0:T(8,128)(2,1)} %queries_hbm.1, bf16[256,128]{1,0:T(8,128)(2,1)} %keys_hbm.1, bf16[256,128]{1,0:T(8,128)(2,1)} %values_hbm.1, bf16[768,384]{1,0:T(8,128)(2,1)} %w_out_hbm.1, bf16[384]{0:T(512)(128)(2,1)} %gain_hbm.1, ...), custom_call_target="tpu_custom_call" | custom-call | tf_op jit(solution)/shard_map/layer/pallas_call | solution.py:770
  182.9 1.6 copy.13

commit v7 on v6

--- a/solution.py
+++ b/solution.py
@@ -82,6 +82,11 @@
 
     def arrived(self, number, dst, device):
         self.copy(number, dst, dst, device).wait_recv()
+
+    def sent(self, copies):
+        for copy in copies:
+            copy.wait_send()
+        self.open = [copy for copy in self.open if all(copy is not other for other in copies)]
 
     def finish(self):
         for copy in self.open:
@@ -456,6 +461,8 @@
     def chosen(x, target):
         return partial.at[x, pl.ds(0, 2), target]
 
+    groups = {}
+
     def send_group(g):
         x = wrapped(place.x + g)
         for zh in range(2):
@@ -470,7 +477,13 @@
             number = 208 + FAR_FIRST.index(g) * 8 + step
             link.send(number, chosen(x, target), token_rows.at[place.tp, x], place.tp_peer(step))
         token_rows[place.tp, x] = chosen(x, place.tp)[...]
-
+        groups[g] = link.open[-7:]
+
+    flow.far_done(1)
+    flow.near2(1, 2)
+    send_group(0)
+    for g in (0, 1, -1):
+        flow.far2(1, g)
     for step in range(1, 16):
         source = lax.rem(place.member + 16 - step, 16)
         link.arrived(88 + step, gains.at[source], members[15 - step])
@@ -483,18 +496,15 @@
             return rows.at[x, z, pl.ds(part * 4, 4)]
         return rows.at[x, z, pl.ds(part * 4 + half * 2, 2)]
 
-    def first_group():
-        flow.far_done(1)
-        flow.near2(1, 2)
-        send_group(0)
-        for g in (0, 1, -1, 2):
-            flow.far2(1, g)
-
-    def more_groups():
+    def middle_groups():
+        flow.far2(1, 2)
+        send_group(1)
+
+    def next_group():
         for g in (0, 1, -1, 2):
             flow.far2_done(1, g)
-        for g in (1, -1, 2):
-            send_group(g)
+        link.sent(groups[0])
+        send_group(-1)
         gate_acc[...] = jnp.zeros_like(gate_acc)
         up_acc[...] = jnp.zeros_like(up_acc)
         row_squares[...] = jnp.zeros_like(row_squares)
@@ -510,6 +520,9 @@
             loads[9].wait()
             loads[10].wait()
         if part == 2:
+            if along == 0:
+                link.sent(groups[1])
+                send_group(2)
             use_tokens(along)
             return
         z = wrapped(place.z + along)
@@ -555,7 +568,7 @@
                 right = jnp.concatenate([weights[span, :] for span in spans], axis=0)
                 acc[:, x] += jnp.dot(left, right, preferred_element_type=F32).reshape(2, 96, 512)
 
-    plane_gather(Gather(place, link, block_of_rows, 112), busy=first_group, later=more_groups, seen=use_rows)
+    plane_gather(Gather(place, link, block_of_rows, 112), busy=middle_groups, later=next_group, seen=use_rows)
     link.finish()
     for zh in range(2):
         mean = jnp.sum(row_squares[zh].reshape(384, 128), axis=1, keepdims=True) / D
@@ -608,6 +621,7 @@
             number = 260 + FAR_FIRST.index(g) * 8 + step
             link.send(number, token_rows.at[target, x], back_rows.at[place.tp, x], place.tp_peer(step))
         back_rows[place.tp, x] = token_rows[place.tp, x]
+        groups[g] = link.open[-7:]
 
     def weigh(g):
         x = wrapped(place.x + g)
@@ -709,25 +723,30 @@
     over_z = Ring(296, "z", cell, lambda step, d: cell(step, pl.ds(d * 128, 128)), z_half, z_part)
 
     for g in FAR_FIRST:
-        send_back(g)
+        if g in (2, 1):
+            send_back(g)
         for part in (0, 1):
             compute(part, g)
             outer[part][g].far()
     for g in (2, 1, -1):
         for part in (0, 1):
             outer[part][g].near()
-    weigh(2)
-    over_x.far()
+    link.sent(groups[2])
+    send_back(-1)
     for part in (0, 1):
         outer[part][2].end()
         inner[part].far()
     for part in (0, 1):
         outer[part][0].near()
-    weigh(1)
+    weigh(2)
+    over_x.far()
     for part in (0, 1):
         outer[part][1].end()
         outer[part][-1].end()
         inner[part].near()
+    link.sent(groups[1])
+    send_back(0)
+    weigh(1)
     weigh(-1)
     over_x.near()
     base = 192

time: 187 us -> 181 us (0.968)
  Pallas kernels: 183 us -> 178 us
    pallas_call x1, Pallas kernels: 183 us -> 178 us  [on_device(): pl.pallas_call(layer_kernel, out_shape=jax.ShapeDtypeStruct((256, 384), B...]
where the time goes in v7:
time: 181 us; the launch traced here: 179 us
  Pallas kernels  178 us (98%)
    pallas_call x1, Pallas kernels, on_device(): pl.pallas_call(layer_kernel, out_shape=jax.ShapeDtypeStruct((256, 384), B...  178 us

profile of v7, /device:TPU:1, one launch (start us, length us, event | category | flops | bytes accessed | tf_op | source)
XLA Modules:
  0.0 179.2 jit_solution(2422962324833807236)
XLA Ops:
  0.0 177.6 %layer.1 = bf16[256,384]{1,0:T(8,128)(2,1)} custom-call(bf16[256,384]{1,0:T(8,128)(2,1)} %resid_hbm.1, bf16[256,768]{1,0:T(8,128)(2,1)} %queries_hbm.1, bf16[256,128]{1,0:T(8,128)(2,1)} %keys_hbm.1, bf16[256,128]{1,0:T(8,128)(2,1)} %values_hbm.1, bf16[768,384]{1,0:T(8,128)(2,1)} %w_out_hbm.1, bf16[384]{0:T(512)(128)(2,1)} %gain_hbm.1, ...), custom_call_target="tpu_custom_call" | custom-call | tf_op jit(solution)/shard_map/layer/pallas_call | solution.py:789
  177.6 1.6 copy.13

commit v8 on v7

--- a/solution.py
+++ b/solution.py
@@ -723,16 +723,18 @@
     over_z = Ring(296, "z", cell, lambda step, d: cell(step, pl.ds(d * 128, 128)), z_half, z_part)
 
     for g in FAR_FIRST:
-        if g in (2, 1):
+        if g == 2:
             send_back(g)
         for part in (0, 1):
             compute(part, g)
             outer[part][g].far()
-    for g in (2, 1, -1):
+    for part in (0, 1):
+        outer[part][2].near()
+    link.sent(groups[2])
+    send_back(1)
+    for g in (1, -1):
         for part in (0, 1):
             outer[part][g].near()
-    link.sent(groups[2])
-    send_back(-1)
     for part in (0, 1):
         outer[part][2].end()
         inner[part].far()
@@ -740,13 +742,15 @@
         outer[part][0].near()
     weigh(2)
     over_x.far()
+    link.sent(groups[1])
+    send_back(-1)
     for part in (0, 1):
         outer[part][1].end()
         outer[part][-1].end()
         inner[part].near()
-    link.sent(groups[1])
+    weigh(1)
+    link.sent(groups[-1])
     send_back(0)
-    weigh(1)
     weigh(-1)
     over_x.near()
     base = 192

time: 181 us -> 179 us (0.989)
  Pallas kernels: 178 us -> 176 us
    pallas_call x1, Pallas kernels: 178 us -> 176 us  [on_device(): pl.pallas_call(layer_kernel, out_shape=jax.ShapeDtypeStruct((256, 384), B...]
where the time goes in v8:
time: 179 us; the launch traced here: 177 us
  Pallas kernels  176 us (98%)
    pallas_call x1, Pallas kernels, on_device(): pl.pallas_call(layer_kernel, out_shape=jax.ShapeDtypeStruct((256, 384), B...  176 us

profile of v8, /device:TPU:1, one launch (start us, length us, event | category | flops | bytes accessed | tf_op | source)
XLA Modules:
  0.0 177.4 jit_solution(1743095857934134168)
XLA Ops:
  0.0 175.7 %layer.1 = bf16[256,384]{1,0:T(8,128)(2,1)} custom-call(bf16[256,384]{1,0:T(8,128)(2,1)} %resid_hbm.1, bf16[256,768]{1,0:T(8,128)(2,1)} %queries_hbm.1, bf16[256,128]{1,0:T(8,128)(2,1)} %keys_hbm.1, bf16[256,128]{1,0:T(8,128)(2,1)} %values_hbm.1, bf16[768,384]{1,0:T(8,128)(2,1)} %w_out_hbm.1, bf16[384]{0:T(512)(128)(2,1)} %gain_hbm.1, ...), custom_call_target="tpu_custom_call" | custom-call | tf_op jit(solution)/shard_map/layer/pallas_call | solution.py:793
  175.8 1.6 copy.13
